TPU v7x, 128 devices: a whole 4x4x4 slice. The times are simulated.
128 devices in a mesh: gx: 4 (over x_lo, core), gy: 8 (over x_hi, y), gz: 4 (over z).
Axes of the slice: x: 4 (x_hi: 2, x_lo: 2; x = x_hi * 2 + x_lo), y: 4, z: 4, core: 2. Of those that a mesh axis runs over, the one named last changes fastest.
Arguments:
- magnetization: float32 [3, 64, 256, 512], P(None, 'gx', 'gy', 'gz'), may hold values from -1 to 1, as said below
- kernel: float32 [6, 256, 512, 64], P(None, ('gx', 'gz'), 'gy'), may hold values from -3 to 3, as said below
- applied: float32 [3], replicated, may hold values from -4 to 4
Outputs:
- predicted: float32 [3, 64, 256, 512], P(None, 'gx', 'gy', 'gz')
- torque: float32 [3, 64, 256, 512], P(None, 'gx', 'gy', 'gz')
Inputs may be any that keep to these rules, and one draw needn't show every extreme that they name: `magnetization`: each cell's three components form a vector of unit length. The tensor is even in wavenumber: kernel[c, ky, kz, kx] equals kernel[c, (256 - ky) mod 256, (512 - kz) mod 512, (64 - kx) mod 64].
All inputs are finite; a program needn't handle non-finite values.
Results may differ from a plain program's by a relative error of at most 0.00011.
Values sent between devices are 32-bit elements; how exact they have to be, the bound alone decides.
A program may use at most 128 MiB of HBM per device.

v0:
```python
import math

import jax
import jax.numpy as jnp
import numpy as np
from jax import lax
from jax.experimental import pallas as pl
from jax.experimental.pallas import tpu as pltpu
from jax.sharding import PartitionSpec as P

MESH = pl.DeviceIdType.MESH
F32 = jnp.float32
BF16 = jnp.bfloat16
NX, NY, NZ = 64, 256, 512
EXCHANGE = 1.0
DAMPING = 0.3
STEP = 0.2
INVERSE_COUNT = 1.0 / (NX * NY * NZ)


def wave_z(block, slot):
    return 64 * block + slot + (block >= 4)


def turn(rows, cols, length):
    angle = 2.0 * np.pi / length * ((rows[:, None] * cols[None, :]) % length)
    return np.cos(angle), np.sin(angle)


def z_tables():
    block, part, slot = (a.reshape(-1) for a in np.meshgrid(np.arange(8), np.arange(2), np.arange(32), indexing="ij"))
    cosine, sine = turn(np.arange(NZ), wave_z(block, slot), NZ)
    forward = np.where(part == 0, cosine, -sine)
    alternate = 1.0 - 2.0 * (np.arange(NZ) % 2)
    packed = (block == 0) & (slot == 0)
    forward[:, packed & (part == 1)] = alternate[:, None]
    backward = np.where(packed, 1.0, 2.0)[:, None] * forward.T
    return forward, backward


def y_tables():
    part, group, owner, tile = (
        a.reshape(-1) for a in np.meshgrid(np.arange(2), np.arange(4), np.arange(16), np.arange(4), indexing="ij")
    )
    ky = 16 * owner + 4 * tile + group
    block, yp, row = (a.reshape(-1) for a in np.meshgrid(np.arange(8), np.arange(2), np.arange(32), indexing="ij"))
    y = 32 * block + row
    cosine, sine = turn(ky, y, NY)
    out_re, in_re = (part == 0)[:, None], (yp == 0)[None, :]
    forward = np.where(out_re == in_re, cosine, np.where(out_re, sine, -sine))
    backward = np.where(out_re == in_re, cosine, np.where(in_re, -sine, sine)).T
    low, high = ((ky > 0) & (ky < 128))[:, None], (ky > 128)[:, None]
    single = np.where(out_re, cosine, -sine)
    forward_packed = np.where(
        low, np.where(in_re, single, 0.0), np.where(high, np.where(in_re, 0.0, single), forward)
    )
    double = 2.0 * single
    backward_packed = np.where(
        low, np.where(in_re, double, 0.0), np.where(high, np.where(in_re, 0.0, double), backward.T)
    ).T
    return forward, forward_packed, backward, backward_packed


def x_tables():
    part, kx = (a.reshape(-1) for a in np.meshgrid(np.arange(2), np.arange(64), indexing="ij"))
    owner, xp, xs = (a.reshape(-1) for a in np.meshgrid(np.arange(16), np.arange(2), np.arange(4), indexing="ij"))
    cosine, sine = turn(kx, 4 * owner + xs, NX)
    out_re, in_re = (part == 0)[:, None], (xp == 0)[None, :]
    forward = np.where(out_re == in_re, cosine, np.where(out_re, sine, -sine))
    mirrored = np.where(in_re, forward, -forward)
    backward = np.where(out_re == in_re, cosine, np.where(in_re, -sine, sine)).T
    return forward, mirrored, backward


def eigen_tables():
    lam = lambda k, n: 2.0 * np.cos(2.0 * np.pi * k / n) - 2.0
    table = np.zeros((16, 8, 4, 128))
    for owner in range(16):
        for block in range(8):
            for tile in range(4):
                for group in range(4):
                    ky = 16 * owner + 4 * tile + group
                    kz = wave_z(block, np.arange(32))
                    row = lam(ky, NY) + lam(kz, NZ)
                    if block == 0:
                        row[0] = lam(ky, NY) + (-2.0 if ky % 128 == 0 else (-4.0 if ky > 128 else 0.0))
                    table[owner, block, tile, 32 * group : 32 * group + 32] = row
    return (
        (table * EXCHANGE).reshape(128, 4, 128).astype(np.float32),
        np.broadcast_to((lam(np.arange(64), NX) * EXCHANGE)[:, None], (64, 128)).astype(np.float32),
    )


def halves(table):
    table = np.asarray(table, np.float64)
    high = table.astype(np.float32).astype(jnp.bfloat16)
    low = (table - high.astype(np.float64)).astype(np.float32).astype(jnp.bfloat16)
    return np.stack([high, low])


def split(value):
    high = value.astype(BF16)
    return high, (value - high.astype(F32)).astype(BF16)


def dot(a, b):
    return jnp.dot(a, b, preferred_element_type=F32)


def right_product(value, table, index, cols):
    high, low = split(value)
    t_high, t_low = table[index, 0, :, cols], table[index, 1, :, cols]
    return dot(high, t_high) + dot(low, t_high) + dot(high, t_low)


def left_product(table, index, rows, high, low):
    t_high, t_low = table[index, 0, rows, :], table[index, 1, rows, :]
    return dot(t_high, high) + dot(t_high, low) + dot(t_low, high)


def swap_lanes(values):
    lane = lax.broadcasted_iota(jnp.int32, values[0].shape, 1)
    low_half = lane < 64
    even = (lane & 32) == 0
    v0, v1, v2, v3 = values
    roll = lambda v, s: pltpu.roll(v, s, 1)
    a0 = jnp.where(low_half, v0, roll(v2, 64))
    a2 = jnp.where(low_half, roll(v0, 64), v2)
    a1 = jnp.where(low_half, v1, roll(v3, 64))
    a3 = jnp.where(low_half, roll(v1, 64), v3)
    return (
        jnp.where(even, a0, roll(a1, 32)),
        jnp.where(even, roll(a0, 96), a1),
        jnp.where(even, a2, roll(a3, 32)),
        jnp.where(even, roll(a2, 96), a3),
    )


PAIR = ((0, 3, 4), (3, 1, 5), (4, 5, 2))
ZF, ZB, YF, YFP, YB, YBP = range(6)
XF, XM, XB = range(3)


def body(
    m_hbm, k_hbm, applied, tab_hbm, tabx_hbm, lam_hbm, lamx_hbm,
    pred_hbm, torque_hbm,
    m, kraw, tab, tabx, lam, lamx, kp, k2, kn_out, kn_in,
    r1, s2, r2, s3, r3, spec, s4, r4, s5, r5, s6, r6, pout, tout,
    local_sem, send_sem, recv_sem, kn_sems,
):
    gx, gy, gz = lax.axis_index("gx"), lax.axis_index("gy"), lax.axis_index("gz")
    ac = gx * 4 + gz
    loads = [
        pltpu.make_async_copy(m_hbm, m, local_sem.at[0]),
        pltpu.make_async_copy(tab_hbm, tab, local_sem.at[1]),
        pltpu.make_async_copy(k_hbm, kraw, local_sem.at[2]),
        pltpu.make_async_copy(tabx_hbm, tabx, local_sem.at[3]),
        pltpu.make_async_copy(lam_hbm.at[ac * 8 + gy], lam, local_sem.at[4]),
        pltpu.make_async_copy(lamx_hbm, lamx, local_sem.at[5]),
    ]
    for load in loads:
        load.start()

    by_z = lambda p: {"gz": p}
    by_y = lambda p: {"gy": p}
    by_xz = lambda p: {"gx": p // 4, "gz": lax.rem(p, 4)}

    barrier = pltpu.get_barrier_semaphore()

    def greet(count, me, place):
        def one(j, carry):
            pl.semaphore_signal(
                barrier, inc=1, device_id=place(lax.rem(me + j, count)), device_id_type=MESH
            )
            return carry

        lax.fori_loop(1, count, one, 0)

    greet(16, ac, by_xz)
    greet(8, gy, by_y)
    pl.semaphore_wait(barrier, 22)

    def copy(e, c, src, dst, device):
        return pltpu.make_async_remote_copy(
            src_ref=src, dst_ref=dst, send_sem=send_sem.at[e, c], recv_sem=recv_sem.at[e, c],
            device_id=device, device_id_type=MESH,
        )

    def send_all(e, c, src, dst, count, me, place):
        def one(j, carry):
            p = lax.rem(me + j, count)
            copy(e, c, src.at[c, p], dst.at[c, me], place(p)).start()
            return carry

        lax.fori_loop(1, count, one, 0)
        dst[c, me] = src[c, me]

    def arrived(e, c, dst, count):
        part = dst.at[c, pl.ds(0, count - 1)]
        copy(e, c, part, part, by_y(lax.rem(gy + 1, 8))).wait_recv()

    def each(step):
        def one(c, carry):
            step(c)
            return carry

        lax.fori_loop(0, 3, one, 0)

    loads[0].wait()
    each(lambda c: send_all(0, c, m, r1, 4, gz, by_z))

    loads[2].wait()

    @pl.when(gy == 4)
    def _():
        for cc in range(6):
            for i in range(16):
                kn_out[cc, i : i + 1, 0:64] = kraw[cc, i, 0:1, :]

    kn = pltpu.make_async_remote_copy(
        src_ref=kn_out, dst_ref=kn_in, send_sem=kn_sems.at[0], recv_sem=kn_sems.at[1],
        device_id=by_y(0), device_id_type=MESH,
    )

    @pl.when(gy == 4)
    def _():
        kn.start()

    for load in loads[1:2] + loads[3:]:
        load.wait()

    def z_forward(c):
        arrived(0, c, r1, 4)
        rows = jnp.concatenate([r1[c, s] for s in range(4)], axis=1)
        for h in range(2):
            out = right_product(rows, tab, ZF, pl.ds(256 * h, 256))
            for u in range(2):
                t = 2 * h + u
                parts = swap_lanes([out[32 * x : 32 * x + 32, 128 * u : 128 * u + 128] for x in range(4)])
                for q in range(4):
                    s2[c, 2 * t + q // 2, 32 * (q % 2) : 32 * (q % 2) + 32, :] = parts[q]
        send_all(1, c, s2, r2, 8, gy, by_y)

    each(z_forward)

    late = (gy >= 4).astype(jnp.int32)
    first = gy == 0

    @pl.when(first)
    def _():
        kn.wait_recv()

    far = first & (ac >= 8)
    middle = first & (lax.rem(ac, 8) == 0)

    def prepare(cc, carry):
        for v in range(4):
            blocks = []
            for g in range(4):
                i = 4 * v + g
                plain = kraw[cc, i, 0:32, :]
                shifted = kraw[cc, i, 1:33, :]
                block = jnp.where(late == 1, shifted, plain)
                row = lax.broadcasted_iota(jnp.int32, block.shape, 0)
                nyquist = jnp.broadcast_to(kn_in[cc, i : i + 1, 0:64], block.shape)
                nyquist = jnp.where(first, nyquist, block)
                if i == 0:
                    top = jnp.where(far, nyquist, block)
                    top = jnp.where(middle, 0.5 * (block + nyquist), top)
                    half = jnp.where(middle & (row == 0), 0.5 * (block - nyquist), 0.0)
                    half = jnp.concatenate([half, jnp.zeros((96, 64), F32)], axis=0)
                    k2[cc] = -INVERSE_COUNT * half.T
                else:
                    top = jnp.where(far, nyquist, block)
                blocks.append(jnp.where(row == 0, top, block))
            kp[cc, v] = -INVERSE_COUNT * jnp.concatenate(blocks, axis=0).T
        return carry

    lax.fori_loop(0, 6, prepare, 0)
    lane = lax.broadcasted_iota(jnp.int32, (64, 128), 1)
    corner = jnp.where(middle & (lane == 0), 2.0 * EXCHANGE * INVERSE_COUNT, 0.0)
    for cc in range(3):
        k2[cc] += corner
        for v in range(4):
            kp[cc, v] += INVERSE_COUNT * (lamx[...] + lam[v : v + 1, :])

    s3_blocks = s3.reshape(3, 16, 32, 128)
    r4_blocks = r4.reshape(3, 16, 32, 128)
    packed_lane = lambda shape: first & ((lax.broadcasted_iota(jnp.int32, shape, 1) & 31) == 0)

    def y_forward(c):
        arrived(1, c, r2, 8)
        high, low = split(r2[c].reshape(512, 128))
        for part in range(2):
            rows = pl.ds(256 * part, 256)
            out = left_product(tab, YF, rows, high, low)
            other = left_product(tab, YFP, rows, high, low)
            out = jnp.where(packed_lane(out.shape), other, out)
            parts = swap_lanes([out[64 * g : 64 * g + 64, :] for g in range(4)])
            for x in range(4):
                s3[c, pl.ds(4 * part + x, 64, stride=8), :] = parts[x]
        send_all(2, c, s3_blocks, r3, 16, ac, by_xz)

    each(y_forward)

    def x_forward(c):
        arrived(2, c, r3, 16)
        for v in range(4):
            high, low = split(r3[c, :, 8 * v : 8 * v + 8, :].reshape(128, 128))
            spec[c, v] = left_product(tabx, XF, pl.ds(0, 128), high, low)
            if v == 0:
                spec[c, 4] = left_product(tabx, XM, pl.ds(0, 128), high, low)

    each(x_forward)

    for c in range(3):
        for v in range(4):
            terms = []
            for part in range(2):
                rows = slice(64 * part, 64 * part + 64)
                total = sum(kp[PAIR[c][d], v] * spec[d, v, rows, :] for d in range(3))
                if v == 0:
                    total = total + sum(k2[PAIR[c][d]] * spec[d, 4, rows, :] for d in range(3))
                terms.append(total)
            high, low = split(jnp.concatenate(terms, axis=0))
            out = left_product(tabx, XB, pl.ds(0, 128), high, low)
            s4[c, :, 8 * v : 8 * v + 8, :] = out.reshape(16, 8, 128)
        send_all(3, c, s4, r4_blocks, 16, ac, by_xz)

    def y_backward(c):
        arrived(3, c, r4_blocks, 16)
        pieces = []
        for part in range(2):
            pieces += swap_lanes([r4[c, pl.ds(4 * part + x, 64, stride=8), :] for x in range(4)])
        high, low = split(jnp.concatenate(pieces, axis=0))
        for h in range(2):
            rows = pl.ds(256 * h, 256)
            out = left_product(tab, YB, rows, high, low)
            other = left_product(tab, YBP, rows, high, low)
            out = jnp.where(packed_lane(out.shape), other, out)
            s5[c, 4 * h : 4 * h + 4] = out.reshape(4, 64, 128)
        send_all(4, c, s5, r5, 8, gy, by_y)

    each(y_backward)

    def z_backward(c):
        arrived(4, c, r5, 8)
        tiles = []
        for t in range(4):
            parts = swap_lanes([r5[c, 2 * t + q // 2, 32 * (q % 2) : 32 * (q % 2) + 32, :] for q in range(4)])
            tiles.append(jnp.concatenate(parts, axis=0))
        rows = jnp.concatenate(tiles, axis=1)
        for h in range(2):
            out = right_product(rows, tab, ZB, pl.ds(256 * h, 256))
            s6[c, 2 * h] = out[:, 0:128]
            s6[c, 2 * h + 1] = out[:, 128:256]
        send_all(5, c, s6, r6, 4, gz, by_z)

    each(z_backward)
    each(lambda c: arrived(5, c, r6, 4))

    def finish(n, carry):
        s, piece = n // 4, lax.rem(n, 4)
        rows = pl.ds(32 * piece, 32)
        mag = [m[c, s, rows, :] for c in range(3)]
        field = [r6[c, s, rows, :] + applied[c] for c in range(3)]
        cross = lambda a, b: [
            a[1] * b[2] - a[2] * b[1],
            a[2] * b[0] - a[0] * b[2],
            a[0] * b[1] - a[1] * b[0],
        ]
        precess = cross(mag, field)
        twist = cross(mag, precess)
        torque = [-(precess[c] + DAMPING * twist[c]) / (1.0 + DAMPING * DAMPING) for c in range(3)]
        stepped = [mag[c] + STEP * torque[c] for c in range(3)]
        length = jnp.sqrt(stepped[0] * stepped[0] + stepped[1] * stepped[1] + stepped[2] * stepped[2])
        for c in range(3):
            tout[c, s, rows, :] = torque[c]
            pout[c, s, rows, :] = stepped[c] / length
        return carry

    lax.fori_loop(0, 16, finish, 0)
    stores = [
        pltpu.make_async_copy(pout, pred_hbm, local_sem.at[0]),
        pltpu.make_async_copy(tout, torque_hbm, local_sem.at[1]),
    ]
    for store in stores:
        store.start()

    def sent(e, src, count):
        def one(c, carry):
            part = src.at[c, pl.ds(0, count - 1)]
            copy(e, c, part, part, by_y(lax.rem(gy + 1, 8))).wait_send()
            return carry

        lax.fori_loop(0, 3, one, 0)

    sent(0, m, 4)
    sent(1, s2, 8)
    sent(2, s3_blocks, 16)
    sent(3, s4, 16)
    sent(4, s5, 8)
    sent(5, s6, 4)

    @pl.when(gy == 4)
    def _():
        kn.wait_send()

    for store in stores:
        store.wait()


def shards(magnetization, kernel, applied):
    tab = np.stack([halves(t) for t in (*z_tables(), *y_tables())])
    tabx = np.stack([halves(t) for t in x_tables()])
    lam, lamx = eigen_tables()
    block = (3, 4, 128, 128)
    anywhere = pl.BlockSpec(memory_space=pl.ANY)
    vmem = lambda *shape, dtype=F32: pltpu.VMEM(shape, dtype)
    predicted, torque = pl.pallas_call(
        body,
        out_shape=[jax.ShapeDtypeStruct(block, F32)] * 2,
        in_specs=[anywhere, anywhere, pl.BlockSpec(memory_space=pltpu.SMEM)] + [anywhere] * 4,
        out_specs=[anywhere] * 2,
        scratch_shapes=[
            vmem(*block),
            vmem(6, 16, 64, 64),
            vmem(6, 2, 512, 512, dtype=BF16),
            vmem(3, 2, 128, 128, dtype=BF16),
            vmem(4, 128),
            vmem(64, 128),
            vmem(6, 4, 64, 128),
            vmem(6, 64, 128),
            vmem(6, 16, 128),
            vmem(6, 16, 128),
            vmem(*block),
            vmem(3, 8, 64, 128),
            vmem(3, 8, 64, 128),
            vmem(3, 512, 128),
            vmem(3, 16, 32, 128),
            vmem(3, 5, 128, 128),
            vmem(3, 16, 32, 128),
            vmem(3, 512, 128),
            vmem(3, 8, 64, 128),
            vmem(3, 8, 64, 128),
            vmem(*block),
            vmem(*block),
            vmem(*block),
            vmem(*block),
            pltpu.SemaphoreType.DMA((6,)),
            pltpu.SemaphoreType.DMA((6, 3)),
            pltpu.SemaphoreType.DMA((6, 3)),
            pltpu.SemaphoreType.DMA((2,)),
        ],
        compiler_params=pltpu.CompilerParams(
            collective_id=0, has_side_effects=True, vmem_limit_bytes=56 * 1024 * 1024
        ),
    )(
        magnetization.reshape(block), kernel, applied,
        jnp.asarray(tab), jnp.asarray(tabx), jnp.asarray(lam), jnp.asarray(lamx),
    )
    shape = magnetization.shape
    return predicted.reshape(shape), torque.reshape(shape)


def solution(mesh):
    return jax.shard_map(
        shards,
        mesh=mesh,
        in_specs=(P(None, "gx", "gy", "gz"), P(None, ("gx", "gz"), "gy", None), P()),
        out_specs=(P(None, "gx", "gy", "gz"), P(None, "gx", "gy", "gz")),
        check_vma=False,
    )
```

profile of v0, /device:TPU:0, one launch (start us, length us, event | category | flops | bytes accessed | tf_op | source)
XLA Modules:
  0.0 67.2 jit_solution(8364979773286707755)
XLA Ops:
  0.6 62.4 %shard_map.86 = (f32[3,4,128,128]{3,2,1,0:T(8,128)}, f32[3,4,128,128]{3,2,1,0:T(8,128)}) custom-call(f32[3,4,128,128]{3,2,1,0:T(8,128)} %bitcast.5, f32[6,16,64,64]{3,2,1,0:T(8,128)} %k_hbm.1, f32[3]{0:T(128)} %applied.1, bf16[6,2,512,512]{3,2,1,0:T(8,128)(2,1)} %constant.8.clone.tab_hbm, bf16[3,2,128,128]{3,2,1,0:T(8,128)(2,1)} %constant.9.clone.tabx_hbm, ...), custom_call_target="tpu_custom_call" | custom-call | tf_op jit(solution)/shard_map/pallas_call | solution.py:420
  63.0 2.1 %copy.11 = f32[3,16,32,128]{3,2,1,0:T(8,128)} copy(f32[3,16,32,128]{3,2,1,0:T(8,128)} %bitcast.4) | data formatting | bytes 1572864
  65.1 2.1 %copy.12 = f32[3,16,32,128]{3,2,1,0:T(8,128)} copy(f32[3,16,32,128]{3,2,1,0:T(8,128)} %bitcast.3) | data formatting | bytes 1572864
where the time goes:
time: 67.4 us; the launch traced here: 67.2 us
  Pallas kernels  62.4 us (93%)
  local copies, waits for them, and re-layouts  4.13 us (6%)
    pallas_call x1, Pallas kernels, shards(): pl.pallas_call(body, out_shape=[jax.ShapeDtypeStruct(block, F32)] * 2, in...  62.4 us
    unnamed x2, local copies, waits for them, and re-layouts  4.13 us

commit v1 on v0

v1 whole, which is shorter than its diff:
```python
import math

import jax
import jax.numpy as jnp
import numpy as np
from jax import lax
from jax.experimental import pallas as pl
from jax.experimental.pallas import tpu as pltpu
from jax.sharding import PartitionSpec as P

MESH = pl.DeviceIdType.MESH
F32 = jnp.float32
BF16 = jnp.bfloat16
NX, NY, NZ = 64, 256, 512
EXCHANGE = 1.0
DAMPING = 0.3
STEP = 0.2
INVERSE_COUNT = 1.0 / (NX * NY * NZ)


def wave_z(block, slot):
    odd = slot >= 16
    return 64 * block + 2 * (slot % 16) + np.where(odd, 1, np.where(block >= 4, 2, 0))


def turn(rows, cols, length):
    angle = 2.0 * np.pi / length * ((rows[:, None] * cols[None, :]) % length)
    return np.cos(angle), np.sin(angle)


def grid(*counts):
    return [a.reshape(-1) for a in np.meshgrid(*(np.arange(n) for n in counts), indexing="ij")]


def z_tables():
    forward, backward = [], []
    for parity in range(2):
        block, part, slot = grid(8, 2, 16)
        cosine, sine = turn(np.arange(NZ // 2), wave_z(block, slot + 16 * parity), NZ)
        table = np.where(part == 0, cosine, -sine)
        weight = np.full(256, 2.0)
        if parity == 0:
            packed = (block == 0) & (slot == 0)
            alternate = 1.0 - 2.0 * (np.arange(NZ // 2) % 2)
            table[:, packed & (part == 1)] = alternate[:, None]
            weight[packed] = 1.0
        forward.append(table)
        backward.append(weight[:, None] * table.T)
    return forward, backward


def y_tables():
    forward, backward = [], []
    for parity in range(2):
        part, group, owner, tile = grid(2, 2, 16, 4)
        ky = 16 * owner + 4 * tile + 2 * group + parity
        half, block, yp, row = grid(2, 4, 2, 16)
        cosine, sine = turn(ky, 32 * block + 16 * half + row, NY)
        out_re, in_re = (part == 0)[:, None], (yp == 0)[None, :]
        plain = np.where(out_re == in_re, cosine, np.where(out_re, sine, -sine))
        low, high = ((ky > 0) & (ky < 128))[:, None], (ky > 128)[:, None]
        single = np.where(out_re, cosine, -sine)
        packed = np.where(low, np.where(in_re, single, 0.0), np.where(high, np.where(in_re, 0.0, single), plain))
        weight = np.where(low | high, 2.0, 1.0)
        forward.append(np.concatenate([plain, packed], axis=0))
        backward.append(np.concatenate([plain.T, (weight * packed).T], axis=0))
    return forward, backward


def x_tables():
    part, kx = grid(2, 64)
    owner, xp, xs = grid(16, 2, 4)
    cosine, sine = turn(kx, 4 * owner + xs, NX)
    out_re, in_re = (part == 0)[:, None], (xp == 0)[None, :]
    forward = np.where(out_re == in_re, cosine, np.where(out_re, sine, -sine))
    mirrored = np.where(in_re, forward, -forward)
    backward = np.where(out_re == in_re, cosine, np.where(in_re, -sine, sine)).T
    return forward, mirrored, backward


def eigen_tables():
    lam = lambda k, n: 2.0 * np.cos(2.0 * np.pi * k / n) - 2.0
    table = np.zeros((16, 8, 4, 128))
    for owner in range(16):
        for block in range(8):
            for tile in range(4):
                for group in range(4):
                    ky = 16 * owner + 4 * tile + group
                    kz = wave_z(block, np.arange(32))
                    row = lam(ky, NY) + lam(kz, NZ)
                    if block == 0:
                        row[0] = lam(ky, NY) + (-2.0 if ky % 128 == 0 else (-4.0 if ky > 128 else 0.0))
                    table[owner, block, tile, 32 * group : 32 * group + 32] = row
    return (
        (table * EXCHANGE).reshape(128, 4, 128).astype(np.float32),
        np.broadcast_to((lam(np.arange(64), NX) * EXCHANGE)[:, None], (64, 128)).astype(np.float32),
    )


def halves(table):
    table = np.asarray(table, np.float64)
    high = table.astype(np.float32).astype(jnp.bfloat16)
    low = (table - high.astype(np.float64)).astype(np.float32).astype(jnp.bfloat16)
    return np.stack([high, low])


def split(value):
    high = value.astype(BF16)
    return high, (value - high.astype(F32)).astype(BF16)


def dot(a, b):
    return jnp.dot(a, b, preferred_element_type=F32)


def right_product(value, table, index):
    high, low = split(value)
    rows = value.shape[0]
    both = dot(jnp.concatenate([high, low], axis=0), table[index, 0])
    return both[:rows] + both[rows:] + dot(high, table[index, 1])


def left_product(table, index, value):
    high, low = split(value)
    cols = value.shape[1]
    both = dot(table[index, 0], jnp.concatenate([high, low], axis=1))
    return both[:, :cols] + both[:, cols:] + dot(table[index, 1], high)


def swap_lanes(values):
    values = list(values)
    lane = lax.broadcasted_iota(jnp.int32, values[0].shape, 1)
    step = len(values) // 2
    width = 64
    while step:
        low = (lane & width) == 0
        for i in range(len(values)):
            if i & step == 0:
                a, b = values[i], values[i + step]
                values[i] = jnp.where(low, a, pltpu.roll(b, width, 1))
                values[i + step] = jnp.where(low, pltpu.roll(a, 128 - width, 1), b)
        step //= 2
        width //= 2
    return values


PAIR = ((0, 3, 4), (3, 1, 5), (4, 5, 2))
FORWARD, BACKWARD = 0, 2
XF, XM, XB = range(3)


def transform(
    m_hbm, k_hbm, tabz_hbm, taby_hbm, tabx_hbm, lam_hbm, lamx_hbm,
    m, r6,
    kraw, tabz, tabyf, tabyb, tabx, lam, lamx, kp, k2, kn_out, kn_in,
    r1, s2, r2, s3, r3, spec, s4, r4, s5, r5, s6,
    local_sem, send_sem, recv_sem, kn_sems,
):
    gx, gy, gz = lax.axis_index("gx"), lax.axis_index("gy"), lax.axis_index("gz")
    ac = gx * 4 + gz
    load_m = pltpu.make_async_copy(m_hbm, m, local_sem.at[0])
    load_m.start()

    by_z = lambda p: {"gz": p}
    by_y = lambda p: {"gy": p}
    by_xz = lambda p: {"gx": p // 4, "gz": lax.rem(p, 4)}

    barrier = pltpu.get_barrier_semaphore()

    def repeat(start, stop, step):
        def one(j, carry):
            step(j)
            return carry

        lax.fori_loop(start, stop, one, 0)

    def greet(count, me, place):
        repeat(
            1,
            count,
            lambda j: pl.semaphore_signal(
                barrier, inc=1, device_id=place(lax.rem(me + j, count)), device_id_type=MESH
            ),
        )

    greet(16, ac, by_xz)
    greet(8, gy, by_y)
    pl.semaphore_wait(barrier, 22)

    def copy(e, n, src, dst, device):
        return pltpu.make_async_remote_copy(
            src_ref=src, dst_ref=dst, send_sem=send_sem.at[e, n], recv_sem=recv_sem.at[e, n],
            device_id=device, device_id_type=MESH,
        )

    def send_all(e, n, src, dst, count, me, place):
        def one(j):
            p = lax.rem(me + j, count)
            copy(e, n, src.at[n, p], dst.at[n, me], place(p)).start()

        repeat(1, count, one)
        dst[n, me] = src[n, me]

    def arrived(e, n, dst, count):
        part = dst.at[n, pl.ds(0, count - 1)]
        copy(e, n, part, part, by_y(lax.rem(gy + 1, 8))).wait_recv()

    load_m.wait()
    m_blocks = m.reshape(3, 4, 4, 32, 128)

    def send_m(n):
        c, half = n // 2, lax.rem(n, 2)
        rows = pl.ds(pl.multiple_of(16 * half, 16), 16)

        def one(j):
            p = lax.rem(gz + j, 4)
            copy(0, n, m_blocks.at[c, p, :, rows, :], r1.at[n, gz], by_z(p)).start()

        repeat(1, 4, one)
        r1[n, gz] = m_blocks[c, gz, :, rows, :]

    repeat(0, 6, send_m)

    loads = [
        pltpu.make_async_copy(tabz_hbm, tabz, local_sem.at[0]),
        pltpu.make_async_copy(k_hbm, kraw, local_sem.at[1]),
        pltpu.make_async_copy(lam_hbm.at[ac * 8 + gy], lam, local_sem.at[2]),
        pltpu.make_async_copy(lamx_hbm, lamx, local_sem.at[3]),
        pltpu.make_async_copy(taby_hbm.at[0:2], tabyf, local_sem.at[4]),
        pltpu.make_async_copy(tabx_hbm, tabx, local_sem.at[5]),
        pltpu.make_async_copy(taby_hbm.at[2:4], tabyb, local_sem.at[6]),
    ]
    for load in loads:
        load.start()

    loads[1].wait()

    @pl.when(gy == 4)
    def _():
        for cc in range(6):
            for i in range(16):
                kn_out[cc, i : i + 1, 0:64] = kraw[cc, i, 0:1, :]

    kn = pltpu.make_async_remote_copy(
        src_ref=kn_out, dst_ref=kn_in, send_sem=kn_sems.at[0], recv_sem=kn_sems.at[1],
        device_id=by_y(0), device_id_type=MESH,
    )

    @pl.when(gy == 4)
    def _():
        kn.start()

    loads[0].wait()

    def z_forward(n):
        arrived(0, n, r1, 4)
        near = [r1[n, s].reshape(64, 128) for s in range(2)]
        far = [r1[n, s + 2].reshape(64, 128) for s in range(2)]
        out = [
            right_product(jnp.concatenate([a + b for a, b in zip(near, far)], axis=1), tabz, FORWARD),
            right_product(jnp.concatenate([a - b for a, b in zip(near, far)], axis=1), tabz, FORWARD + 1),
        ]
        for t in range(2):
            parts = swap_lanes(
                [out[i % 2][16 * (i // 2) : 16 * (i // 2) + 16, 128 * t : 128 * t + 128] for i in range(8)]
            )
            for q in range(8):
                s2[n, 4 * t + q // 2, 16 * (q % 2) : 16 * (q % 2) + 16, :] = parts[q]
        send_all(1, n, s2, r2, 8, gy, by_y)

    repeat(0, 3, z_forward)

    late = (gy >= 4).astype(jnp.int32)
    first = gy == 0

    @pl.when(first)
    def _():
        kn.wait_recv()

    for load in loads[2:4]:
        load.wait()
    far = first & (ac >= 8)
    middle = first & (lax.rem(ac, 8) == 0)

    def prepare(cc):
        for v in range(4):
            blocks = []
            for g in range(4):
                i = 4 * v + g
                even = kraw[cc, i, pl.ds(0, 16, stride=2), :]
                even = jnp.where(late == 1, kraw[cc, i, pl.ds(2, 16, stride=2), :], even)
                block = jnp.concatenate([even, kraw[cc, i, pl.ds(1, 16, stride=2), :]], axis=0)
                row = lax.broadcasted_iota(jnp.int32, block.shape, 0)
                nyquist = jnp.broadcast_to(kn_in[cc, i : i + 1, 0:64], block.shape)
                nyquist = jnp.where(first, nyquist, block)
                top = jnp.where(far, nyquist, block)
                if i == 0:
                    top = jnp.where(middle, 0.5 * (block + nyquist), top)
                    half = jnp.where(middle & (row == 0), 0.5 * (block - nyquist), 0.0)
                    half = jnp.concatenate([half, jnp.zeros((96, 64), F32)], axis=0)
                    k2[cc] = -INVERSE_COUNT * half.T
                blocks.append(jnp.where(row == 0, top, block))
            kp[cc, v] = -INVERSE_COUNT * jnp.concatenate(blocks, axis=0).T

    repeat(0, 6, prepare)
    lane = lax.broadcasted_iota(jnp.int32, (64, 128), 1)
    corner = jnp.where(middle & (lane == 0), 2.0 * EXCHANGE * INVERSE_COUNT, 0.0)
    for cc in range(3):
        k2[cc] += corner
        for v in range(4):
            kp[cc, v] += INVERSE_COUNT * (lamx[...] + lam[v : v + 1, :])

    repeat(3, 6, z_forward)

    for load in loads[4:]:
        load.wait()
    packed_lane = first & ((lax.broadcasted_iota(jnp.int32, (256, 128), 1) & 31) == 0)

    def y_forward(c):
        arrived(1, 2 * c, r2, 8)
        arrived(1, 2 * c + 1, r2, 8)
        both = [r2[pl.ds(2 * c, 2), 4 * h : 4 * h + 4].reshape(256, 128) for h in range(2)]
        out = []
        for parity, value in enumerate((both[0] + both[1], both[0] - both[1])):
            rows = left_product(tabyf, parity, value)
            out.append(jnp.where(packed_lane, rows[256:], rows[:256]))
        for part in range(2):
            at = [128 * part + 64 * (g // 2) for g in range(4)]
            parts = swap_lanes([out[g % 2][at[g] : at[g] + 64] for g in range(4)])
            for x in range(4):
                s3[c, pl.ds(4 * part + x, 64, stride=8), :] = parts[x]
        send_all(2, c, s3_blocks, r3, 16, ac, by_xz)

    s3_blocks = s3.reshape(3, 16, 32, 128)
    r4_blocks = r4.reshape(3, 16, 32, 128)
    repeat(0, 3, y_forward)

    def x_forward(c):
        arrived(2, c, r3, 16)
        tiles = [r3[c, :, 8 * v : 8 * v + 8, :].reshape(128, 128) for v in range(4)]
        for v in range(4):
            spec[c, v] = left_product(tabx, XF, tiles[v])
        spec[c, 4] = left_product(tabx, XM, tiles[0])

    repeat(0, 3, x_forward)

    for c in range(3):
        for v in range(4):
            terms = []
            for part in range(2):
                rows = slice(64 * part, 64 * part + 64)
                total = sum(kp[PAIR[c][d], v] * spec[d, v, rows, :] for d in range(3))
                if v == 0:
                    total = total + sum(k2[PAIR[c][d]] * spec[d, 4, rows, :] for d in range(3))
                terms.append(total)
            out = left_product(tabx, XB, jnp.concatenate(terms, axis=0))
            s4[c, :, 8 * v : 8 * v + 8, :] = out.reshape(16, 8, 128)
        send_all(3, c, s4, r4_blocks, 16, ac, by_xz)

    def y_backward(c):
        arrived(3, c, r4_blocks, 16)
        pieces = [
            swap_lanes([r4[c, pl.ds(4 * part + x, 64, stride=8), :] for x in range(4)]) for part in range(2)
        ]
        out = []
        for parity in range(2):
            value = [pieces[part][2 * g + parity] for part in range(2) for g in range(2)]
            rows = left_product(tabyb, parity, jnp.concatenate(value, axis=0))
            out.append(jnp.where(packed_lane, rows[256:], rows[:256]))
        for h, value in enumerate((out[0] + out[1], out[0] - out[1])):
            s5[pl.ds(2 * c, 2), 4 * h : 4 * h + 4] = value.reshape(2, 4, 32, 128)
        send_all(4, 2 * c, s5, r5, 8, gy, by_y)
        send_all(4, 2 * c + 1, s5, r5, 8, gy, by_y)

    repeat(0, 3, y_backward)

    def z_backward(n):
        arrived(4, n, r5, 8)
        tiles = [[], []]
        for t in range(2):
            parts = swap_lanes(
                [r5[n, 4 * t + q // 2, 16 * (q % 2) : 16 * (q % 2) + 16, :] for q in range(8)]
            )
            for parity in range(2):
                tiles[parity].append(jnp.concatenate(parts[parity::2], axis=0))
        out = [right_product(jnp.concatenate(tiles[p], axis=1), tabz, BACKWARD + p) for p in range(2)]
        for h, value in enumerate((out[0] + out[1], out[0] - out[1])):
            s6[n, 2 * h] = value[:, 0:128]
            s6[n, 2 * h + 1] = value[:, 128:256]
        send_all(5, n, s6, r6, 4, gz, by_z)

    repeat(0, 6, z_backward)
    repeat(0, 6, lambda n: arrived(5, n, r6, 4))

    def sent(e, src, chunks, count):
        def one(n):
            part = src.at[n, pl.ds(0, count - 1)]
            copy(e, n, part, part, by_y(lax.rem(gy + 1, 8))).wait_send()

        repeat(0, chunks, one)

    sent(0, r1, 6, 4)
    sent(1, s2, 6, 8)
    sent(2, s3_blocks, 3, 16)
    sent(3, s4, 3, 16)
    sent(4, s5, 6, 8)
    sent(5, s6, 6, 4)

    @pl.when(gy == 4)
    def _():
        kn.wait_send()


def advance(m, demag, applied, pred_hbm, torque_hbm, pout, tout, sems):
    cross = lambda a, b: [
        a[1] * b[2] - a[2] * b[1],
        a[2] * b[0] - a[0] * b[2],
        a[0] * b[1] - a[1] * b[0],
    ]
    stores = []
    for s in range(4):
        planes = slice(4 * s, 4 * s + 4)
        for half in range(2):
            rows = slice(16 * half, 16 * half + 16)
            mag = [m[c, planes, rows, :] for c in range(3)]
            field = [demag[2 * c + half, s].reshape(4, 16, 128) + applied[c] for c in range(3)]
            precess = cross(mag, field)
            twist = cross(mag, precess)
            torque = [-(precess[c] + DAMPING * twist[c]) / (1.0 + DAMPING * DAMPING) for c in range(3)]
            stepped = [mag[c] + STEP * torque[c] for c in range(3)]
            length = jnp.sqrt(stepped[0] * stepped[0] + stepped[1] * stepped[1] + stepped[2] * stepped[2])
            for c in range(3):
                tout[c, planes, rows, :] = torque[c]
                pout[c, planes, rows, :] = stepped[c] / length
        stores += [
            pltpu.make_async_copy(tout.at[:, planes], torque_hbm.at[:, planes], sems.at[s, 0]),
            pltpu.make_async_copy(pout.at[:, planes], pred_hbm.at[:, planes], sems.at[s, 1]),
        ]
        stores[-2].start()
        stores[-1].start()
    for store in stores:
        store.wait()


def shards(magnetization, kernel, applied):
    zf, zb = z_tables()
    yf, yb = y_tables()
    tabz = np.stack([halves(t) for t in zf + zb])
    taby = np.stack([halves(t) for t in yf + yb])
    tabx = np.stack([halves(t) for t in x_tables()])
    lam, lamx = eigen_tables()
    shape = magnetization.shape
    anywhere = pl.BlockSpec(memory_space=pltpu.HBM)
    in_vmem = pl.BlockSpec(memory_space=pltpu.VMEM)
    vmem = lambda *shape, dtype=F32: pltpu.VMEM(shape, dtype)
    m, demag = pl.pallas_call(
        transform,
        out_shape=[vmem(*shape), vmem(6, 4, 64, 128)],
        in_specs=[anywhere] * 7,
        out_specs=[in_vmem, in_vmem],
        scratch_shapes=[
            vmem(6, 16, 64, 64),
            vmem(4, 2, 256, 256, dtype=BF16),
            vmem(2, 2, 512, 256, dtype=BF16),
            vmem(2, 2, 512, 256, dtype=BF16),
            vmem(3, 2, 128, 128, dtype=BF16),
            vmem(4, 128),
            vmem(64, 128),
            vmem(6, 4, 64, 128),
            vmem(6, 64, 128),
            vmem(6, 16, 128),
            vmem(6, 16, 128),
            vmem(6, 4, 4, 16, 128),
            vmem(6, 8, 32, 128),
            vmem(6, 8, 32, 128),
            vmem(3, 512, 128),
            vmem(3, 16, 32, 128),
            vmem(3, 5, 128, 128),
            vmem(3, 16, 32, 128),
            vmem(3, 512, 128),
            vmem(6, 8, 32, 128),
            vmem(6, 8, 32, 128),
            vmem(6, 4, 64, 128),
            pltpu.SemaphoreType.DMA((7,)),
            pltpu.SemaphoreType.DMA((6, 6)),
            pltpu.SemaphoreType.DMA((6, 6)),
            pltpu.SemaphoreType.DMA((2,)),
        ],
        compiler_params=pltpu.CompilerParams(
            collective_id=0, has_side_effects=True, vmem_limit_bytes=40 * 1024 * 1024
        ),
    )(
        magnetization, kernel, jnp.asarray(tabz), jnp.asarray(taby), jnp.asarray(tabx),
        jnp.asarray(lam), jnp.asarray(lamx),
    )
    return pl.pallas_call(
        advance,
        out_shape=[jax.ShapeDtypeStruct(shape, F32)] * 2,
        in_specs=[in_vmem, in_vmem, pl.BlockSpec(memory_space=pltpu.SMEM)],
        out_specs=[anywhere] * 2,
        scratch_shapes=[vmem(*shape), vmem(*shape), pltpu.SemaphoreType.DMA((4, 2))],
        compiler_params=pltpu.CompilerParams(vmem_limit_bytes=16 * 1024 * 1024),
    )(m, demag, applied)


def solution(mesh):
    return jax.shard_map(
        shards,
        mesh=mesh,
        in_specs=(P(None, "gx", "gy", "gz"), P(None, ("gx", "gz"), "gy", None), P()),
        out_specs=(P(None, "gx", "gy", "gz"), P(None, "gx", "gy", "gz")),
        check_vma=False,
    )
```

time: 67.4 us -> 69.4 us (1.030)
  local copies, waits for them, and re-layouts: 4.13 us -> 8.47 us
  Pallas kernels: 62.4 us -> 59.9 us
    unnamed x2 -> x16, local copies, waits for them, and re-layouts: 4.13 us -> 8.47 us
    pallas_call x1 -> x2, Pallas kernels: 62.4 us -> 59.9 us  [the longest x1 58 us: shards(): pl.pallas_call(transform, out_shape=[vmem(*shape), vmem(6, 4, 64, 128)],...]
where the time goes in v1:
time: 69.4 us; the launch traced here: 69 us
  Pallas kernels  59.9 us (86%)
  local copies, waits for them, and re-layouts  8.47 us (12%)
    pallas_call x1, Pallas kernels, shards(): pl.pallas_call(transform, out_shape=[vmem(*shape), vmem(6, 4, 64, 128)],...  58 us
    unnamed x16, local copies, waits for them, and re-layouts  8.47 us
    pallas_call x1, Pallas kernels, shards(): pl.pallas_call(advance, out_shape=[jax.ShapeDtypeStruct(shape, F32)] * 2,...  1.83 us

profile of v1, /device:TPU:0, one launch (start us, length us, event | category | flops | bytes accessed | tf_op | source)
XLA Modules:
  0.0 69.0 jit_solution(1407765038807258421)
XLA Ops:
  0.6 0.0 copy-start
  0.6 1.9 %copy-done = f32[6,16,64,64]{3,2,1,0:T(8,128)S(1)} copy-done((f32[6,16,64,64]{3,2,1,0:T(8,128)S(1)}, f32[6,16,64,64]{3,2,1,0:T(8,128)}, u32[]{:S(2)}) %copy-start) | copy-done | bytes 1572888
  2.5 0.0 copy-start.1
  2.5 1.6 %copy-done.1 = bf16[4,2,512,256]{3,2,1,0:T(8,128)(2,1)S(1)} copy-done((bf16[4,2,512,256]{3,2,1,0:T(8,128)(2,1)S(1)}, bf16[4,2,512,256]{3,2,1,0:T(8,128)(2,1)}, u32[]{:S(2)}) %copy-start.1) | copy-done | bytes 2097176
  4.1 0.0 copy-start.2
  4.1 1.2 %copy-done.2 = bf16[4,2,256,256]{3,2,1,0:T(8,128)(2,1)S(1)} copy-done((bf16[4,2,256,256]{3,2,1,0:T(8,128)(2,1)S(1)}, bf16[4,2,256,256]{3,2,1,0:T(8,128)(2,1)}, u32[]{:S(2)}) %copy-start.2) | copy-done | bytes 1048600
  5.3 0.0 copy-start.3
  5.3 1.1 %copy-done.3 = f32[3,16,32,128]{3,2,1,0:T(8,128)S(1)} copy-done((f32[3,16,32,128]{3,2,1,0:T(8,128)S(1)}, f32[3,16,32,128]{3,2,1,0:T(8,128)}, u32[]{:S(2)}) %copy-start.3) | copy-done | bytes 786456
  6.5 0.0 copy-start.4
  6.5 0.9 %copy-done.4 = f32[128,4,128]{2,1,0:T(4,128)S(1)} copy-done((f32[128,4,128]{2,1,0:T(4,128)S(1)}, f32[128,4,128]{2,1,0:T(4,128)}, u32[]{:S(2)}) %copy-start.4) | copy-done | bytes 262168
  7.4 0.0 copy-start.5
  7.4 0.9 %copy-done.5 = bf16[3,2,128,128]{3,2,1,0:T(8,128)(2,1)S(1)} copy-done((bf16[3,2,128,128]{3,2,1,0:T(8,128)(2,1)S(1)}, bf16[3,2,128,128]{3,2,1,0:T(8,128)(2,1)}, u32[]{:S(2)}) %copy-start.5) | copy-done | bytes 196632
  8.3 0.0 copy-start.6
  8.4 0.8 %copy-done.6 = f32[64,128]{1,0:T(8,128)S(1)} copy-done((f32[64,128]{1,0:T(8,128)S(1)}, f32[64,128]{1,0:T(8,128)}, u32[]{:S(2)}) %copy-start.6) | copy-done | bytes 32792
  9.1 0.0 copy-start.7
  9.1 58.0 %shard_map.95 = (f32[3,16,32,128]{3,2,1,0:T(8,128)S(1)}, f32[6,4,64,128]{3,2,1,0:T(8,128)S(1)}) custom-call(f32[3,16,32,128]{3,2,1,0:T(8,128)S(1)} %copy-done.3, f32[6,16,64,64]{3,2,1,0:T(8,128)S(1)} %copy-done, bf16[4,2,256,256]{3,2,1,0:T(8,128)(2,1)S(1)} %copy-done.2, bf16[4,2,512,256]{3,2,1,0:T(8,128)(2,1)S(1)} %copy-done.1, ...), custom_call_target="tpu_custom_call" | custom-call | tf_op jit(solution)/shard_map/pallas_call | solution.py:456
  67.1 0.0 copy-done.7
  67.2 1.8 %shard_map.96 = (f32[3,16,32,128]{3,2,1,0:T(8,128)}, f32[3,16,32,128]{3,2,1,0:T(8,128)}) custom-call(f32[3,16,32,128]{3,2,1,0:T(8,128)S(1)} %get-tuple-element.4.m, f32[6,4,64,128]{3,2,1,0:T(8,128)S(1)} %get-tuple-element.5.demag, f32[3]{0:T(128)S(1)} %copy-done.7), custom_call_target="tpu_custom_call" | custom-call | tf_op jit(solution)/shard_map/pallas_call | solution.py:496
Async XLA Ops:
  0.6 1.9 %copy-start = (f32[6,16,64,64]{3,2,1,0:T(8,128)S(1)}, f32[6,16,64,64]{3,2,1,0:T(8,128)}, u32[]{:S(2)}) copy-start(f32[6,16,64,64]{3,2,1,0:T(8,128)} %k_hbm.1) | copy-start | bytes 4718596
  2.5 1.6 %copy-start.1 = (bf16[4,2,512,256]{3,2,1,0:T(8,128)(2,1)S(1)}, bf16[4,2,512,256]{3,2,1,0:T(8,128)(2,1)}, u32[]{:S(2)}) copy-start(bf16[4,2,512,256]{3,2,1,0:T(8,128)(2,1)} %constant.11.clone.taby_hbm) | copy-start | bytes 6291460
  4.1 1.2 %copy-start.2 = (bf16[4,2,256,256]{3,2,1,0:T(8,128)(2,1)S(1)}, bf16[4,2,256,256]{3,2,1,0:T(8,128)(2,1)}, u32[]{:S(2)}) copy-start(bf16[4,2,256,256]{3,2,1,0:T(8,128)(2,1)} %constant.10.clone.tabz_hbm) | copy-start | bytes 3145732
  5.3 1.1 %copy-start.3 = (f32[3,16,32,128]{3,2,1,0:T(8,128)S(1)}, f32[3,16,32,128]{3,2,1,0:T(8,128)}, u32[]{:S(2)}) copy-start(f32[3,16,32,128]{3,2,1,0:T(8,128)} %m_hbm.1) | copy-start | bytes 2359300
  6.5 0.9 %copy-start.4 = (f32[128,4,128]{2,1,0:T(4,128)S(1)}, f32[128,4,128]{2,1,0:T(4,128)}, u32[]{:S(2)}) copy-start(f32[128,4,128]{2,1,0:T(4,128)} %constant.13.clone.lam_hbm) | copy-start | bytes 786436
  7.4 0.9 %copy-start.5 = (bf16[3,2,128,128]{3,2,1,0:T(8,128)(2,1)S(1)}, bf16[3,2,128,128]{3,2,1,0:T(8,128)(2,1)}, u32[]{:S(2)}) copy-start(bf16[3,2,128,128]{3,2,1,0:T(8,128)(2,1)} %constant.12.clone.tabx_hbm) | copy-start | bytes 589828
  8.3 0.8 %copy-start.6 = (f32[64,128]{1,0:T(8,128)S(1)}, f32[64,128]{1,0:T(8,128)}, u32[]{:S(2)}) copy-start(f32[64,128]{1,0:T(8,128)} %constant.14.clone.lamx_hbm) | copy-start | bytes 98308
  9.1 58.0 %copy-start.7 = (f32[3]{0:T(128)S(1)}, f32[3]{0:T(128)}, u32[]{:S(2)}) copy-start(f32[3]{0:T(128)} %applied.1) | copy-start | bytes 40

commit v2 on v1

--- a/solution.py
+++ b/solution.py
@@ -487,7 +487,7 @@
             pltpu.SemaphoreType.DMA((2,)),
         ],
         compiler_params=pltpu.CompilerParams(
-            collective_id=0, has_side_effects=True, vmem_limit_bytes=40 * 1024 * 1024
+            collective_id=0, has_side_effects=True, vmem_limit_bytes=62 * 1024 * 1024
         ),
     )(
         magnetization, kernel, jnp.asarray(tabz), jnp.asarray(taby), jnp.asarray(tabx),

time: 69.4 us -> 60.7 us (0.87)
  local copies, waits for them, and re-layouts: 8.47 us -> 0.01 us
    unnamed x16 -> x2, local copies, waits for them, and re-layouts: 8.47 us -> 0.01 us
where the time goes in v2:
time: 60.7 us; the launch traced here: 60.6 us
  Pallas kernels  59.9 us (99%)
  between operations  0.65 us (1%)
    pallas_call x1, Pallas kernels, shards(): pl.pallas_call(transform, out_shape=[vmem(*shape), vmem(6, 4, 64, 128)],...  58.1 us
    pallas_call x1, Pallas kernels, shards(): pl.pallas_call(advance, out_shape=[jax.ShapeDtypeStruct(shape, F32)] * 2,...  1.83 us

profile of v2, /device:TPU:0, one launch (start us, length us, event | category | flops | bytes accessed | tf_op | source)
XLA Modules:
  0.0 60.6 jit_solution(8391580963761184528)
XLA Ops:
  0.6 0.0 copy-start
  0.6 58.1 %shard_map.95 = (f32[3,16,32,128]{3,2,1,0:T(8,128)S(1)}, f32[6,4,64,128]{3,2,1,0:T(8,128)S(1)}) custom-call(f32[3,16,32,128]{3,2,1,0:T(8,128)} %m_hbm.1, f32[6,16,64,64]{3,2,1,0:T(8,128)} %k_hbm.1, bf16[4,2,256,256]{3,2,1,0:T(8,128)(2,1)} %constant.10.clone.tabz_hbm, bf16[4,2,512,256]{3,2,1,0:T(8,128)(2,1)} %constant.11.clone.taby_hbm, ...), custom_call_target="tpu_custom_call" | custom-call | tf_op jit(solution)/shard_map/pallas_call | solution.py:456
  58.7 0.0 copy-done
  58.7 1.8 %shard_map.96 = (f32[3,16,32,128]{3,2,1,0:T(8,128)}, f32[3,16,32,128]{3,2,1,0:T(8,128)}) custom-call(f32[3,16,32,128]{3,2,1,0:T(8,128)S(1)} %get-tuple-element.4.m, f32[6,4,64,128]{3,2,1,0:T(8,128)S(1)} %get-tuple-element.5.demag, f32[3]{0:T(128)S(1)} %copy-done), custom_call_target="tpu_custom_call" | custom-call | tf_op jit(solution)/shard_map/pallas_call | solution.py:496
Async XLA Ops:
  0.6 58.1 %copy-start = (f32[3]{0:T(128)S(1)}, f32[3]{0:T(128)}, u32[]{:S(2)}) copy-start(f32[3]{0:T(128)} %applied.1) | copy-start | bytes 40

commit v3 on v2

--- a/solution.py
+++ b/solution.py
@@ -161,9 +161,25 @@
     load_m = pltpu.make_async_copy(m_hbm, m, local_sem.at[0])
     load_m.start()
 
-    by_z = lambda p: {"gz": p}
     by_y = lambda p: {"gy": p}
-    by_xz = lambda p: {"gx": p // 4, "gz": lax.rem(p, 4)}
+    on_z = [(z, {"gz": z}) for z in (lax.rem(gz + d, 4) for d in (2, 1, 3))]
+    on_y = [
+        (y, {"gy": y})
+        for y in (
+            4 * lax.rem(gy // 4 + p, 2) + lax.rem(gy + d, 4)
+            for p, d in ((1, 2), (1, 1), (1, 3), (1, 0), (0, 2), (0, 1), (0, 3))
+        )
+    ]
+    on_xz = [
+        (4 * x + z, {"gx": x, "gz": z})
+        for x, z in (
+            (2 * lax.rem(gx // 2 + p, 2) + lax.rem(gx + k, 2), lax.rem(gz + d, 4))
+            for p in (1, 0)
+            for d in (2, 1, 3, 0)
+            for k in (0, 1)
+            if (p, d, k) != (0, 0, 0)
+        )
+    ]
 
     barrier = pltpu.get_barrier_semaphore()
 
@@ -174,17 +190,8 @@
 
         lax.fori_loop(start, stop, one, 0)
 
-    def greet(count, me, place):
-        repeat(
-            1,
-            count,
-            lambda j: pl.semaphore_signal(
-                barrier, inc=1, device_id=place(lax.rem(me + j, count)), device_id_type=MESH
-            ),
-        )
-
-    greet(16, ac, by_xz)
-    greet(8, gy, by_y)
+    for _, device in on_y + on_xz:
+        pl.semaphore_signal(barrier, inc=1, device_id=device, device_id_type=MESH)
     pl.semaphore_wait(barrier, 22)
 
     def copy(e, n, src, dst, device):
@@ -193,12 +200,9 @@
             device_id=device, device_id_type=MESH,
         )
 
-    def send_all(e, n, src, dst, count, me, place):
-        def one(j):
-            p = lax.rem(me + j, count)
-            copy(e, n, src.at[n, p], dst.at[n, me], place(p)).start()
-
-        repeat(1, count, one)
+    def send_all(e, n, src, dst, me, others):
+        for p, device in others:
+            copy(e, n, src.at[n, p], dst.at[n, me], device).start()
         dst[n, me] = src[n, me]
 
     def arrived(e, n, dst, count):
@@ -212,11 +216,8 @@
         c, half = n // 2, lax.rem(n, 2)
         rows = pl.ds(pl.multiple_of(16 * half, 16), 16)
 
-        def one(j):
-            p = lax.rem(gz + j, 4)
-            copy(0, n, m_blocks.at[c, p, :, rows, :], r1.at[n, gz], by_z(p)).start()
-
-        repeat(1, 4, one)
+        for p, device in on_z:
+            copy(0, n, m_blocks.at[c, p, :, rows, :], r1.at[n, gz], device).start()
         r1[n, gz] = m_blocks[c, gz, :, rows, :]
 
     repeat(0, 6, send_m)
@@ -266,7 +267,7 @@
             )
             for q in range(8):
                 s2[n, 4 * t + q // 2, 16 * (q % 2) : 16 * (q % 2) + 16, :] = parts[q]
-        send_all(1, n, s2, r2, 8, gy, by_y)
+        send_all(1, n, s2, r2, gy, on_y)
 
     repeat(0, 3, z_forward)
 
@@ -329,7 +330,7 @@
             parts = swap_lanes([out[g % 2][at[g] : at[g] + 64] for g in range(4)])
             for x in range(4):
                 s3[c, pl.ds(4 * part + x, 64, stride=8), :] = parts[x]
-        send_all(2, c, s3_blocks, r3, 16, ac, by_xz)
+        send_all(2, c, s3_blocks, r3, ac, on_xz)
 
     s3_blocks = s3.reshape(3, 16, 32, 128)
     r4_blocks = r4.reshape(3, 16, 32, 128)
@@ -355,7 +356,7 @@
                 terms.append(total)
             out = left_product(tabx, XB, jnp.concatenate(terms, axis=0))
             s4[c, :, 8 * v : 8 * v + 8, :] = out.reshape(16, 8, 128)
-        send_all(3, c, s4, r4_blocks, 16, ac, by_xz)
+        send_all(3, c, s4, r4_blocks, ac, on_xz)
 
     def y_backward(c):
         arrived(3, c, r4_blocks, 16)
@@ -369,8 +370,8 @@
             out.append(jnp.where(packed_lane, rows[256:], rows[:256]))
         for h, value in enumerate((out[0] + out[1], out[0] - out[1])):
             s5[pl.ds(2 * c, 2), 4 * h : 4 * h + 4] = value.reshape(2, 4, 32, 128)
-        send_all(4, 2 * c, s5, r5, 8, gy, by_y)
-        send_all(4, 2 * c + 1, s5, r5, 8, gy, by_y)
+        send_all(4, 2 * c, s5, r5, gy, on_y)
+        send_all(4, 2 * c + 1, s5, r5, gy, on_y)
 
     repeat(0, 3, y_backward)
 
@@ -387,10 +388,9 @@
         for h, value in enumerate((out[0] + out[1], out[0] - out[1])):
             s6[n, 2 * h] = value[:, 0:128]
             s6[n, 2 * h + 1] = value[:, 128:256]
-        send_all(5, n, s6, r6, 4, gz, by_z)
+        send_all(5, n, s6, r6, gz, on_z)
 
     repeat(0, 6, z_backward)
-    repeat(0, 6, lambda n: arrived(5, n, r6, 4))
 
     def sent(e, src, chunks, count):
         def one(n):
@@ -404,11 +404,13 @@
     sent(2, s3_blocks, 3, 16)
     sent(3, s4, 3, 16)
     sent(4, s5, 6, 8)
-    sent(5, s6, 6, 4)
 
     @pl.when(gy == 4)
     def _():
         kn.wait_send()
+
+    repeat(0, 6, lambda n: arrived(5, n, r6, 4))
+    sent(5, s6, 6, 4)
 
 
 def advance(m, demag, applied, pred_hbm, torque_hbm, pout, tout, sems):

time: 60.7 us -> 59.7 us (0.984)
  Pallas kernels: 59.9 us -> 58.9 us
    pallas_call x1, Pallas kernels: 58.1 us -> 57.1 us  [shards(): pl.pallas_call(transform, out_shape=[vmem(*shape), vmem(6, 4, 64, 128)],...]
where the time goes in v3:
time: 59.7 us; the launch traced here: 59.6 us
  Pallas kernels  58.9 us (99%)
  between operations  0.65 us (1%)
    pallas_call x1, Pallas kernels, shards(): pl.pallas_call(transform, out_shape=[vmem(*shape), vmem(6, 4, 64, 128)],...  57.1 us
    pallas_call x1, Pallas kernels, shards(): pl.pallas_call(advance, out_shape=[jax.ShapeDtypeStruct(shape, F32)] * 2,...  1.83 us

profile of v3, /device:TPU:0, one launch (start us, length us, event | category | flops | bytes accessed | tf_op | source)
XLA Modules:
  0.0 59.6 jit_solution(18266564861930475871)
XLA Ops:
  0.6 0.0 copy-start
  0.6 57.1 %shard_map.95 = (f32[3,16,32,128]{3,2,1,0:T(8,128)S(1)}, f32[6,4,64,128]{3,2,1,0:T(8,128)S(1)}) custom-call(f32[3,16,32,128]{3,2,1,0:T(8,128)} %m_hbm.1, f32[6,16,64,64]{3,2,1,0:T(8,128)} %k_hbm.1, bf16[4,2,256,256]{3,2,1,0:T(8,128)(2,1)} %constant.10.clone.tabz_hbm, bf16[4,2,512,256]{3,2,1,0:T(8,128)(2,1)} %constant.11.clone.taby_hbm, ...), custom_call_target="tpu_custom_call" | custom-call | tf_op jit(solution)/shard_map/pallas_call | solution.py:458
  57.7 0.0 copy-done
  57.7 1.8 %shard_map.96 = (f32[3,16,32,128]{3,2,1,0:T(8,128)}, f32[3,16,32,128]{3,2,1,0:T(8,128)}) custom-call(f32[3,16,32,128]{3,2,1,0:T(8,128)S(1)} %get-tuple-element.4.m, f32[6,4,64,128]{3,2,1,0:T(8,128)S(1)} %get-tuple-element.5.demag, f32[3]{0:T(128)S(1)} %copy-done), custom_call_target="tpu_custom_call" | custom-call | tf_op jit(solution)/shard_map/pallas_call | solution.py:498
Async XLA Ops:
  0.6 57.1 %copy-start = (f32[3]{0:T(128)S(1)}, f32[3]{0:T(128)}, u32[]{:S(2)}) copy-start(f32[3]{0:T(128)} %applied.1) | copy-start | bytes 40

commit v4 on v3

v4 whole, which is shorter than its diff:
```python
import math

import jax
import jax.numpy as jnp
import numpy as np
from jax import lax
from jax.experimental import pallas as pl
from jax.experimental.pallas import tpu as pltpu
from jax.sharding import PartitionSpec as P

MESH = pl.DeviceIdType.MESH
F32 = jnp.float32
BF16 = jnp.bfloat16
NX, NY, NZ = 64, 256, 512
EXCHANGE = 1.0
DAMPING = 0.3
STEP = 0.2
INVERSE_COUNT = 1.0 / (NX * NY * NZ)


def wave_z(block, slot):
    odd = slot >= 16
    return 64 * block + 2 * (slot % 16) + np.where(odd, 1, np.where(block >= 4, 2, 0))


def turn(rows, cols, length):
    angle = 2.0 * np.pi / length * ((rows[:, None] * cols[None, :]) % length)
    return np.cos(angle), np.sin(angle)


def grid(*counts):
    return [a.reshape(-1) for a in np.meshgrid(*(np.arange(n) for n in counts), indexing="ij")]


def z_tables():
    forward, backward = [], []
    for parity in range(2):
        block, part, slot = grid(8, 2, 16)
        cosine, sine = turn(np.arange(NZ // 2), wave_z(block, slot + 16 * parity), NZ)
        table = np.where(part == 0, cosine, -sine)
        weight = np.full(256, 2.0)
        if parity == 0:
            packed = (block == 0) & (slot == 0)
            alternate = 1.0 - 2.0 * (np.arange(NZ // 2) % 2)
            table[:, packed & (part == 1)] = alternate[:, None]
            weight[packed] = 1.0
        forward.append(table)
        backward.append(weight[:, None] * table.T)
    return forward, backward


def wave_y(owner, tile, group):
    return 128 * (tile // 2) + 16 * owner + 8 * (tile % 2) + group


def y_tables():
    forward, backward = [], []
    for parity in range(2):
        group, owner, tile = grid(4, 8, 4)
        half, block, row = grid(2, 4, 16)
        tables = turn(wave_y(owner, tile, 2 * group + parity), 32 * block + 16 * half + row, NY)
        forward.append(np.concatenate(tables, axis=0))
        backward.append(np.concatenate([t.T for t in tables], axis=0))
    return forward, backward


def x_tables():
    part, kx = grid(2, 64)
    parity, owner, xs, xp = grid(2, 8, 4, 2)
    cosine, sine = turn(kx, 4 * owner + xs, NX)
    out_re, in_re = (part == 0)[:, None], (xp == 0)[None, :]
    mine = kx[:, None] % 2 == parity[None, :]
    forward = np.where(mine, np.where(out_re == in_re, cosine, np.where(out_re, sine, -sine)), 0.0)
    mirrored = np.where(in_re, forward, -forward)
    backward = np.where(mine, np.where(out_re == in_re, cosine, np.where(in_re, -sine, sine)), 0.0).T
    return forward, mirrored, backward


def eigen_tables():
    lam = lambda k, n: 2.0 * np.cos(2.0 * np.pi * k / n) - 2.0
    owner, parity, block, tile, group, slot = grid(8, 2, 8, 4, 8, 16)
    ky, kz = wave_y(owner, tile, group), wave_z(block, slot + 16 * parity)
    z_part = lam(kz, NZ)
    packed = (block == 0) & (parity == 0) & (slot == 0)
    z_part = np.where(packed, np.where(ky % 128 == 0, -2.0, np.where(ky > 128, -4.0, 0.0)), z_part)
    table = (lam(ky, NY) + z_part) * EXCHANGE
    return (
        table.reshape(128, 4, 128).astype(np.float32),
        np.broadcast_to((lam(np.arange(64), NX) * EXCHANGE)[:, None], (64, 128)).astype(np.float32),
    )


def halves(table):
    table = np.asarray(table, np.float64)
    high = table.astype(np.float32).astype(jnp.bfloat16)
    low = (table - high.astype(np.float64)).astype(np.float32).astype(jnp.bfloat16)
    return np.stack([high, low])


def split(value):
    high = value.astype(BF16)
    return high, (value - high.astype(F32)).astype(BF16)


def dot(a, b):
    return jnp.dot(a, b, preferred_element_type=F32)


def right_product(value, table, index):
    high, low = split(value)
    rows = value.shape[0]
    both = dot(jnp.concatenate([high, low], axis=0), table[index, 0])
    return both[:rows] + both[rows:] + dot(high, table[index, 1])


def left_product(table, index, value):
    high, low = split(value)
    cols = value.shape[1]
    both = dot(table[index, 0], jnp.concatenate([high, low], axis=1))
    return both[:, :cols] + both[:, cols:] + dot(table[index, 1], high)


def swap_lanes(values):
    values = list(values)
    lane = lax.broadcasted_iota(jnp.int32, values[0].shape, 1)
    step = len(values) // 2
    width = 64
    while step:
        low = (lane & width) == 0
        for i in range(len(values)):
            if i & step == 0:
                a, b = values[i], values[i + step]
                values[i] = jnp.where(low, a, pltpu.roll(b, width, 1))
                values[i + step] = jnp.where(low, pltpu.roll(a, 128 - width, 1), b)
        step //= 2
        width //= 2
    return values


PAIR = ((0, 3, 4), (3, 1, 5), (4, 5, 2))
FORWARD, BACKWARD = 0, 2
XF, XM, XB = range(3)


def transform(
    m_hbm, k_hbm, tabz_hbm, taby_hbm, tabx_hbm, lam_hbm, lamx_hbm,
    m, r6,
    kraw, tabz, tabyf, tabyb, tabx, lam, lamx, kp, k2, kq, kn_out, kn_in, kr_out, kr_in,
    r1, s2, r2, s3, r3, spec, s4, r4, s5, r5, s6,
    local_sem, send_sem, recv_sem, kn_sems,
):
    gx, gy, gz = lax.axis_index("gx"), lax.axis_index("gy"), lax.axis_index("gz")
    core, top = lax.rem(gx, 2), gx // 2
    place_xy = 2 * gy + top
    place_z = 4 * core + gz
    load_m = pltpu.make_async_copy(m_hbm, m, local_sem.at[0])
    load_m.start()

    by_y = lambda p: {"gy": p}
    on_z = [(z, {"gz": z}) for z in (lax.rem(gz + d, 4) for d in (2, 1, 3))]
    on_xy = [
        (2 * y + x, {"gx": 2 * x + core, "gy": y})
        for y, x in (
            (4 * lax.rem(gy // 4 + p, 2) + lax.rem(gy + d, 4), lax.rem(top + f, 2))
            for p, d, f in (
                (1, 2, 0), (1, 1, 0), (1, 3, 0), (1, 2, 1), (0, 2, 1), (1, 0, 0), (1, 1, 1), (1, 3, 1),
                (0, 1, 1), (0, 3, 1), (0, 2, 0), (1, 0, 1), (0, 0, 1), (0, 1, 0), (0, 3, 0),
            )
        )
    ]
    on_cz = [
        (4 * k + z, {"gx": 2 * top + k, "gz": z})
        for k, z in (
            (lax.rem(core + k, 2), lax.rem(gz + d, 4)) for d in (2, 1, 3, 0) for k in (0, 1) if (d, k) != (0, 0)
        )
    ]

    barrier = pltpu.get_barrier_semaphore()

    def repeat(start, stop, step):
        def one(j, carry):
            step(j)
            return carry

        lax.fori_loop(start, stop, one, 0)

    for _, device in on_xy + on_cz:
        pl.semaphore_signal(barrier, inc=1, device_id=device, device_id_type=MESH)
    pl.semaphore_wait(barrier, 22)

    def copy(e, n, src, dst, device):
        return pltpu.make_async_remote_copy(
            src_ref=src, dst_ref=dst, send_sem=send_sem.at[e, n], recv_sem=recv_sem.at[e, n],
            device_id=device, device_id_type=MESH,
        )

    def send_all(e, n, src, dst, me, others):
        for p, device in others:
            copy(e, n, src.at[n, p], dst.at[n, me], device).start()
        dst[n, me] = src[n, me]

    def arrived(e, n, dst, count):
        part = dst.at[n, pl.ds(0, count - 1)]
        copy(e, n, part, part, by_y(lax.rem(gy + 1, 8))).wait_recv()

    def send_both(e, c, src, dst):
        for p, device in on_cz:
            copy(e, c, src.at[c, :, p], dst.at[c, :, place_z], device).start()
        dst[c, :, place_z] = src[c, :, place_z]

    def both_arrived(e, c, dst):
        part = dst.at[c, :, pl.ds(0, 7)]
        copy(e, c, part, part, by_y(lax.rem(gy + 1, 8))).wait_recv()

    load_m.wait()
    m_blocks = m.reshape(3, 4, 4, 32, 128)

    def send_m(n):
        c, half = n // 2, lax.rem(n, 2)
        rows = pl.ds(pl.multiple_of(16 * half, 16), 16)

        for p, device in on_z:
            copy(0, n, m_blocks.at[c, p, :, rows, :], r1.at[n, gz], device).start()
        r1[n, gz] = m_blocks[c, gz, :, rows, :]

    repeat(0, 6, send_m)

    loads = [
        pltpu.make_async_copy(tabz_hbm, tabz, local_sem.at[0]),
        pltpu.make_async_copy(k_hbm, kraw, local_sem.at[1]),
        pltpu.make_async_copy(lam_hbm.at[(2 * place_z + top) * 8 + gy], lam, local_sem.at[2]),
        pltpu.make_async_copy(lamx_hbm, lamx, local_sem.at[3]),
        pltpu.make_async_copy(taby_hbm.at[0:2], tabyf, local_sem.at[4]),
        pltpu.make_async_copy(tabx_hbm, tabx, local_sem.at[5]),
        pltpu.make_async_copy(taby_hbm.at[2:4], tabyb, local_sem.at[6]),
    ]
    for load in loads:
        load.start()

    loads[1].wait()

    @pl.when(gy == 4)
    def _():
        for cc in range(6):
            for i in range(16):
                kn_out[cc, i : i + 1, 0:64] = kraw[cc, i, 0:1, :]

    kn = pltpu.make_async_remote_copy(
        src_ref=kn_out, dst_ref=kn_in, send_sem=kn_sems.at[0], recv_sem=kn_sems.at[1],
        device_id=by_y(0), device_id_type=MESH,
    )

    @pl.when(gy == 4)
    def _():
        kn.start()

    loads[0].wait()

    def z_forward(n):
        arrived(0, n, r1, 4)
        near = [r1[n, s].reshape(64, 128) for s in range(2)]
        far = [r1[n, s + 2].reshape(64, 128) for s in range(2)]
        out = [
            right_product(jnp.concatenate([a + b for a, b in zip(near, far)], axis=1), tabz, FORWARD),
            right_product(jnp.concatenate([a - b for a, b in zip(near, far)], axis=1), tabz, FORWARD + 1),
        ]
        for parity in range(2):
            for t in range(2):
                parts = swap_lanes(
                    [out[parity][16 * x : 16 * x + 16, 128 * t : 128 * t + 128] for x in range(4)]
                )
                for q in range(4):
                    s2[n, 2 * (4 * t + q) + parity] = parts[q]
        send_all(1, n, s2, r2_blocks, place_xy, on_xy)

    r2_blocks = r2.reshape(6, 16, 16, 128)
    s5_blocks = s5.reshape(6, 16, 16, 128)
    repeat(0, 3, z_forward)

    late = gy >= 4
    first = gy == 0
    middle = first & (place_z == 0)

    @pl.when(first)
    def _():
        kn.wait_recv()

    for load in loads[2:4]:
        load.wait()

    def prepare(cc):
        for v in range(2):
            own, other = [], []
            for g in range(8):
                i = 8 * v + g
                even = kraw[cc, i, pl.ds(0, 16, stride=2), :]
                even = jnp.where(late, kraw[cc, i, pl.ds(2, 16, stride=2), :], even)
                odd = kraw[cc, i, pl.ds(1, 16, stride=2), :]
                row = lax.broadcasted_iota(jnp.int32, even.shape, 0)
                nyquist = jnp.broadcast_to(kn_in[cc, i : i + 1, 0:64], even.shape)
                nyquist = jnp.where(first, nyquist, even)
                packed = jnp.where(top == 1, nyquist, even)
                if i == 0:
                    packed = jnp.where(middle, 0.5 * (even + nyquist), packed)
                    kr_out[cc, 0:1, 0:64] = 0.5 * (even - nyquist)[0:1, :]
                even = jnp.where(row == 0, packed, even)
                own.append(jnp.where(top == 1, odd, even))
                other.append(jnp.where(top == 1, even, odd))
            kp[cc, 2 * top + v] = -INVERSE_COUNT * jnp.concatenate(own, axis=0).T
            kq[cc, v] = -INVERSE_COUNT * jnp.concatenate(other, axis=0).T

    repeat(0, 6, prepare)
    repeat(3, 6, z_forward)

    across = {"gx": lax.rem(gx + 2, 4)}
    shares = [
        pltpu.make_async_remote_copy(
            src_ref=src, dst_ref=dst, send_sem=kn_sems.at[n], recv_sem=kn_sems.at[n + 1],
            device_id=across, device_id_type=MESH,
        )
        for n, src, dst in ((2, kq, kp.at[:, pl.ds(2 * top, 2)]), (4, kr_out, kr_in))
    ]
    for share in shares:
        share.start()

    for load in loads[4:]:
        load.wait()
    row = lax.broadcasted_iota(jnp.int32, (128, 128), 0)
    lane = lax.broadcasted_iota(jnp.int32, (128, 128), 1)
    real = (lane & 16) == 0
    packed_lane = first & (top == 0) & ((lane & 15) == 0)
    low = (row & 2) == 0
    lone = ((row & 125) == 0, row < 0)
    partner = lambda z: jnp.where(real, pltpu.roll(z, 112, 1), pltpu.roll(z, 16, 1))

    def y_forward(c):
        arrived(1, 2 * c, r2_blocks, 16)
        arrived(1, 2 * c + 1, r2_blocks, 16)
        part = lambda h, x: r2[pl.ds(2 * c, 2), 4 * h : 4 * h + 4, x].reshape(128, 128)
        halves_x = []
        for h in range(2):
            a, b = part(h, 0), part(h, 1)
            halves_x.append(jnp.concatenate([a + b, a - b], axis=1))
        out = [[], []]
        for parity, value in enumerate((halves_x[0] + halves_x[1], halves_x[0] - halves_x[1])):
            rows = left_product(tabyf, parity, value)
            for e in range(2):
                cosine, sine = rows[:128, 128 * e : 128 * e + 128], rows[128:, 128 * e : 128 * e + 128]
                turned = partner(sine)
                plain = cosine + jnp.where(real, turned, -turned)
                single = jnp.where(
                    low, jnp.where(real, cosine, -turned), jnp.where(real, partner(cosine), -sine)
                )
                out[e].append(jnp.where(packed_lane & ~lone[parity], single, plain))
        for e in range(2):
            parts = swap_lanes([out[e][g % 2][32 * (g // 2) : 32 * (g // 2) + 32] for g in range(8)])
            for x in range(8):
                s3[c, e, pl.ds(x, 32, stride=8), :] = parts[x]
        send_both(2, c, s3_blocks, r3)

    s3_blocks = s3.reshape(3, 2, 8, 32, 128)
    r4_blocks = r4.reshape(3, 2, 8, 32, 128)
    repeat(0, 3, y_forward)

    def x_forward(c):
        both_arrived(2, c, r3)
        tiles = [r3[c, :, :, 8 * v : 8 * v + 8, :].reshape(128, 128) for v in range(4)]
        for v in range(4):
            spec[c, v] = left_product(tabx, XF, tiles[v])
        for j in range(2):
            spec[c, 4 + j] = left_product(tabx, XM, tiles[2 * j])

    repeat(0, 2, x_forward)

    for share in shares:
        share.wait_recv()
    corner_lane = middle & (top == 0) & (lax.broadcasted_iota(jnp.int32, (64, 128), 1) == 0)
    for cc in range(6):
        for j, source in enumerate((kr_out, kr_in)):
            column = jnp.broadcast_to(source[cc, 0:1, 0:64], (128, 64)).T
            column = -INVERSE_COUNT * column + (2.0 * EXCHANGE * INVERSE_COUNT if cc < 3 else 0.0)
            k2[cc, j] = jnp.where(corner_lane, column, 0.0)
        if cc < 3:
            for v in range(4):
                kp[cc, v] += INVERSE_COUNT * (lamx[...] + lam[v : v + 1, :])
    x_forward(2)

    for c in range(3):
        for v in range(4):
            terms = []
            for part in range(2):
                rows = slice(64 * part, 64 * part + 64)
                total = sum(kp[PAIR[c][d], v] * spec[d, v, rows, :] for d in range(3))
                if v % 2 == 0:
                    total = total + sum(
                        k2[PAIR[c][d], v // 2] * spec[d, 4 + v // 2, rows, :] for d in range(3)
                    )
                terms.append(total)
            out = left_product(tabx, XB, jnp.concatenate(terms, axis=0))
            s4[c, :, :, 8 * v : 8 * v + 8, :] = out.reshape(2, 8, 8, 128)
        send_both(3, c, s4, r4_blocks)

    alternate = (1 - 2 * (row & 1)).astype(F32)

    def y_backward(c):
        both_arrived(3, c, r4_blocks)
        pieces = [swap_lanes([r4[c, e, pl.ds(x, 32, stride=8), :] for x in range(8)]) for e in range(2)]
        out = [[], []]
        for parity in range(2):
            value = [
                jnp.concatenate([pieces[e][2 * g + parity] for g in range(4)], axis=0) for e in range(2)
            ]
            masked = [jnp.where(low & ~lone[parity], z, 0.0) for z in value]
            rows = left_product(tabyb, parity, jnp.concatenate(value, axis=1))
            rows_low = left_product(tabyb, parity, jnp.concatenate(masked, axis=1))
            for e in range(2):
                cols = slice(128 * e, 128 * e + 128)
                cosine, sine = rows[:128, cols], rows[128:, cols]
                cosine_low, sine_low = rows_low[:128, cols], rows_low[128:, cols]
                turned = partner(sine)
                plain = cosine + jnp.where(real, -turned, turned)
                cosine_high, sine_high = cosine - cosine_low, sine - sine_low
                base = 0.0
                if parity == 0:
                    base = value[e][0:1, :] + alternate * value[e][2:3, :]
                    cosine_high = cosine_high - base
                double = jnp.where(real, cosine_low - partner(sine_low), partner(cosine_high) - sine_high)
                out[e].append(jnp.where(packed_lane, 2.0 * double + base, plain))
        for h in range(2):
            even, odd = [out[e][0] + out[e][1] if h == 0 else out[e][0] - out[e][1] for e in range(2)]
            for x, value in enumerate((even + odd, even - odd)):
                s5[pl.ds(2 * c, 2), 4 * h : 4 * h + 4, x] = value.reshape(2, 4, 16, 128)
        send_all(4, 2 * c, s5_blocks, r5, place_xy, on_xy)
        send_all(4, 2 * c + 1, s5_blocks, r5, place_xy, on_xy)

    repeat(0, 3, y_backward)

    def z_backward(n):
        arrived(4, n, r5, 16)
        tiles = [[], []]
        for parity in range(2):
            for t in range(2):
                parts = swap_lanes([r5[n, 2 * (4 * t + q) + parity] for q in range(4)])
                tiles[parity].append(jnp.concatenate(parts, axis=0))
        out = [right_product(jnp.concatenate(tiles[p], axis=1), tabz, BACKWARD + p) for p in range(2)]
        for h, value in enumerate((out[0] + out[1], out[0] - out[1])):
            s6[n, 2 * h] = value[:, 0:128]
            s6[n, 2 * h + 1] = value[:, 128:256]
        send_all(5, n, s6, r6, gz, on_z)

    repeat(0, 6, z_backward)

    def sent(e, chunks, part):
        repeat(0, chunks, lambda n: copy(e, n, part(n), part(n), by_y(lax.rem(gy + 1, 8))).wait_send())

    sent(0, 6, lambda n: r1.at[n, pl.ds(0, 3)])
    sent(1, 6, lambda n: s2.at[n, pl.ds(0, 15)])
    sent(2, 3, lambda n: s3_blocks.at[n, :, pl.ds(0, 7)])
    sent(3, 3, lambda n: s4.at[n, :, pl.ds(0, 7)])
    sent(4, 6, lambda n: s5_blocks.at[n, pl.ds(0, 15)])
    for share in shares:
        share.wait_send()

    @pl.when(gy == 4)
    def _():
        kn.wait_send()

    repeat(0, 6, lambda n: arrived(5, n, r6, 4))
    sent(5, 6, lambda n: s6.at[n, pl.ds(0, 3)])


def advance(m, demag, applied, pred_hbm, torque_hbm, pout, tout, sems):
    cross = lambda a, b: [
        a[1] * b[2] - a[2] * b[1],
        a[2] * b[0] - a[0] * b[2],
        a[0] * b[1] - a[1] * b[0],
    ]
    stores = []
    for s in range(4):
        planes = slice(4 * s, 4 * s + 4)
        for half in range(2):
            rows = slice(16 * half, 16 * half + 16)
            mag = [m[c, planes, rows, :] for c in range(3)]
            field = [demag[2 * c + half, s].reshape(4, 16, 128) + applied[c] for c in range(3)]
            precess = cross(mag, field)
            twist = cross(mag, precess)
            torque = [-(precess[c] + DAMPING * twist[c]) / (1.0 + DAMPING * DAMPING) for c in range(3)]
            stepped = [mag[c] + STEP * torque[c] for c in range(3)]
            length = jnp.sqrt(stepped[0] * stepped[0] + stepped[1] * stepped[1] + stepped[2] * stepped[2])
            for c in range(3):
                tout[c, planes, rows, :] = torque[c]
                pout[c, planes, rows, :] = stepped[c] / length
        stores += [
            pltpu.make_async_copy(tout.at[:, planes], torque_hbm.at[:, planes], sems.at[s, 0]),
            pltpu.make_async_copy(pout.at[:, planes], pred_hbm.at[:, planes], sems.at[s, 1]),
        ]
        stores[-2].start()
        stores[-1].start()
    for store in stores:
        store.wait()


def shards(magnetization, kernel, applied):
    zf, zb = z_tables()
    yf, yb = y_tables()
    tabz = np.stack([halves(t) for t in zf + zb])
    taby = np.stack([halves(t) for t in yf + yb])
    tabx = np.stack([halves(t) for t in x_tables()])
    lam, lamx = eigen_tables()
    shape = magnetization.shape
    anywhere = pl.BlockSpec(memory_space=pltpu.HBM)
    in_vmem = pl.BlockSpec(memory_space=pltpu.VMEM)
    vmem = lambda *shape, dtype=F32: pltpu.VMEM(shape, dtype)
    m, demag = pl.pallas_call(
        transform,
        out_shape=[vmem(*shape), vmem(6, 4, 64, 128)],
        in_specs=[anywhere] * 7,
        out_specs=[in_vmem, in_vmem],
        scratch_shapes=[
            vmem(6, 16, 64, 64),
            vmem(4, 2, 256, 256, dtype=BF16),
            vmem(2, 2, 256, 128, dtype=BF16),
            vmem(2, 2, 256, 128, dtype=BF16),
            vmem(3, 2, 128, 128, dtype=BF16),
            vmem(4, 128),
            vmem(64, 128),
            vmem(6, 4, 64, 128),
            vmem(6, 2, 64, 128),
            vmem(6, 2, 64, 128),
            vmem(6, 16, 128),
            vmem(6, 16, 128),
            vmem(6, 8, 128),
            vmem(6, 8, 128),
            vmem(6, 4, 4, 16, 128),
            vmem(6, 16, 16, 128),
            vmem(6, 8, 2, 16, 128),
            vmem(3, 2, 256, 128),
            vmem(3, 2, 8, 32, 128),
            vmem(3, 6, 128, 128),
            vmem(3, 2, 8, 32, 128),
            vmem(3, 2, 256, 128),
            vmem(6, 8, 2, 16, 128),
            vmem(6, 16, 16, 128),
            vmem(6, 4, 64, 128),
            pltpu.SemaphoreType.DMA((7,)),
            pltpu.SemaphoreType.DMA((6, 6)),
            pltpu.SemaphoreType.DMA((6, 6)),
            pltpu.SemaphoreType.DMA((6,)),
        ],
        compiler_params=pltpu.CompilerParams(
            collective_id=0, has_side_effects=True, vmem_limit_bytes=62 * 1024 * 1024
        ),
    )(
        magnetization, kernel, jnp.asarray(tabz), jnp.asarray(taby), jnp.asarray(tabx),
        jnp.asarray(lam), jnp.asarray(lamx),
    )
    return pl.pallas_call(
        advance,
        out_shape=[jax.ShapeDtypeStruct(shape, F32)] * 2,
        in_specs=[in_vmem, in_vmem, pl.BlockSpec(memory_space=pltpu.SMEM)],
        out_specs=[anywhere] * 2,
        scratch_shapes=[vmem(*shape), vmem(*shape), pltpu.SemaphoreType.DMA((4, 2))],
        compiler_params=pltpu.CompilerParams(vmem_limit_bytes=16 * 1024 * 1024),
    )(m, demag, applied)


def solution(mesh):
    return jax.shard_map(
        shards,
        mesh=mesh,
        in_specs=(P(None, "gx", "gy", "gz"), P(None, ("gx", "gz"), "gy", None), P()),
        out_specs=(P(None, "gx", "gy", "gz"), P(None, "gx", "gy", "gz")),
        check_vma=False,
    )
```

time: 59.7 us -> 58.3 us (0.977); the launches traced: 59.6 us -> 57.4 us
  Pallas kernels: 58.9 us -> 56.7 us
    pallas_call x1, Pallas kernels: 57.1 us -> 54.9 us  [shards(): pl.pallas_call(transform, out_shape=[vmem(*shape), vmem(6, 4, 64, 128)],...]
where the time goes in v4:
time: 58.3 us; the launch traced here: 57.4 us
  Pallas kernels  56.7 us (97%)
  between operations  0.65 us (1%)
    pallas_call x1, Pallas kernels, shards(): pl.pallas_call(transform, out_shape=[vmem(*shape), vmem(6, 4, 64, 128)],...  54.9 us
    pallas_call x1, Pallas kernels, shards(): pl.pallas_call(advance, out_shape=[jax.ShapeDtypeStruct(shape, F32)] * 2,...  1.83 us

profile of v4, /device:TPU:0, one launch (start us, length us, event | category | flops | bytes accessed | tf_op | source)
XLA Modules:
  0.0 57.4 jit_solution(1390854905728149419)
XLA Ops:
  0.6 0.0 copy-start
  0.6 54.9 %shard_map.95 = (f32[3,16,32,128]{3,2,1,0:T(8,128)S(1)}, f32[6,4,64,128]{3,2,1,0:T(8,128)S(1)}) custom-call(f32[3,16,32,128]{3,2,1,0:T(8,128)} %m_hbm.1, f32[6,16,64,64]{3,2,1,0:T(8,128)} %k_hbm.1, bf16[4,2,256,256]{3,2,1,0:T(8,128)(2,1)} %constant.10.clone.tabz_hbm, bf16[4,2,256,128]{3,2,1,0:T(8,128)(2,1)} %constant.11.clone.taby_hbm, ...), custom_call_target="tpu_custom_call" | custom-call | tf_op jit(solution)/shard_map/pallas_call | solution.py:514
  55.5 0.0 copy-done
  55.6 1.8 %shard_map.96 = (f32[3,16,32,128]{3,2,1,0:T(8,128)}, f32[3,16,32,128]{3,2,1,0:T(8,128)}) custom-call(f32[3,16,32,128]{3,2,1,0:T(8,128)S(1)} %get-tuple-element.4.m, f32[6,4,64,128]{3,2,1,0:T(8,128)S(1)} %get-tuple-element.5.demag, f32[3]{0:T(128)S(1)} %copy-done), custom_call_target="tpu_custom_call" | custom-call | tf_op jit(solution)/shard_map/pallas_call | solution.py:557
Async XLA Ops:
  0.6 54.9 %copy-start = (f32[3]{0:T(128)S(1)}, f32[3]{0:T(128)}, u32[]{:S(2)}) copy-start(f32[3]{0:T(128)} %applied.1) | copy-start | bytes 40

commit v5 on v4

--- a/solution.py
+++ b/solution.py
@@ -97,6 +97,11 @@
     return np.stack([high, low])
 
 
+def left_halves(table):
+    high, low = halves(table)
+    return np.concatenate([high, high, low], axis=1)
+
+
 def split(value):
     high = value.astype(BF16)
     return high, (value - high.astype(F32)).astype(BF16)
@@ -114,6 +119,11 @@
 
 
 def left_product(table, index, value):
+    high, low = split(value)
+    return dot(table[index], jnp.concatenate([high, low, high], axis=0))
+
+
+def wide_product(table, index, value):
     high, low = split(value)
     cols = value.shape[1]
     both = dot(table[index, 0], jnp.concatenate([high, low], axis=1))
@@ -145,7 +155,7 @@
 def transform(
     m_hbm, k_hbm, tabz_hbm, taby_hbm, tabx_hbm, lam_hbm, lamx_hbm,
     m, r6,
-    kraw, tabz, tabyf, tabyb, tabx, lam, lamx, kp, k2, kq, kn_out, kn_in, kr_out, kr_in,
+    kraw, tabz, tabyf, tabyb, tabx, lam, lamx, kp, k2, kq, kn_out, kn_in,
     r1, s2, r2, s3, r3, spec, s4, r4, s5, r5, s6,
     local_sem, send_sem, recv_sem, kn_sems,
 ):
@@ -155,6 +165,8 @@
     place_z = 4 * core + gz
     load_m = pltpu.make_async_copy(m_hbm, m, local_sem.at[0])
     load_m.start()
+    load_k = pltpu.make_async_copy(k_hbm, kraw, local_sem.at[1])
+    load_k.start()
 
     by_y = lambda p: {"gy": p}
     on_z = [(z, {"gz": z}) for z in (lax.rem(gz + d, 4) for d in (2, 1, 3))]
@@ -227,7 +239,6 @@
 
     loads = [
         pltpu.make_async_copy(tabz_hbm, tabz, local_sem.at[0]),
-        pltpu.make_async_copy(k_hbm, kraw, local_sem.at[1]),
         pltpu.make_async_copy(lam_hbm.at[(2 * place_z + top) * 8 + gy], lam, local_sem.at[2]),
         pltpu.make_async_copy(lamx_hbm, lamx, local_sem.at[3]),
         pltpu.make_async_copy(taby_hbm.at[0:2], tabyf, local_sem.at[4]),
@@ -237,23 +248,49 @@
     for load in loads:
         load.start()
 
-    loads[1].wait()
+    load_k.wait()
+    late = gy >= 4
+    first = gy == 0
+
+    def prepare(cc):
+        for v in range(2):
+            own, other = [], []
+            for g in range(8):
+                i = 8 * v + g
+                even = kraw[cc, i, pl.ds(0, 16, stride=2), :]
+                even = jnp.where(late, kraw[cc, i, pl.ds(2, 16, stride=2), :], even)
+                odd = kraw[cc, i, pl.ds(1, 16, stride=2), :]
+                own.append(jnp.where(top == 1, odd, even))
+                other.append(jnp.where(top == 1, even, odd))
+            kp[cc, 2 * top + v] = -INVERSE_COUNT * jnp.concatenate(own, axis=0).T
+            kq[cc, v] = -INVERSE_COUNT * jnp.concatenate(other, axis=0).T
+
+    def share(n, start, count):
+        part = pl.ds(start, count)
+        return pltpu.make_async_remote_copy(
+            src_ref=kq.at[part], dst_ref=kp.at[part, pl.ds(2 * top, 2)],
+            send_sem=kn_sems.at[n], recv_sem=kn_sems.at[n + 1],
+            device_id={"gx": lax.rem(gx + 2, 4)}, device_id_type=MESH,
+        )
+
+    shares = [share(0, 0, 2), share(2, 2, 4)]
+    repeat(0, 2, prepare)
+    shares[0].start()
+
+    def nyquist(n):
+        return pltpu.make_async_remote_copy(
+            src_ref=kn_out, dst_ref=kn_in.at[n], send_sem=kn_sems.at[4], recv_sem=kn_sems.at[5 + n],
+            device_id={"gx": core, "gy": 0}, device_id_type=MESH,
+        )
 
     @pl.when(gy == 4)
     def _():
         for cc in range(6):
             for i in range(16):
                 kn_out[cc, i : i + 1, 0:64] = kraw[cc, i, 0:1, :]
-
-    kn = pltpu.make_async_remote_copy(
-        src_ref=kn_out, dst_ref=kn_in, send_sem=kn_sems.at[0], recv_sem=kn_sems.at[1],
-        device_id=by_y(0), device_id_type=MESH,
-    )
-
-    @pl.when(gy == 4)
-    def _():
-        kn.start()
-
+        nyquist(top).start()
+
+    repeat(2, 6, prepare)
     loads[0].wait()
 
     def z_forward(n):
@@ -275,55 +312,10 @@
 
     r2_blocks = r2.reshape(6, 16, 16, 128)
     s5_blocks = s5.reshape(6, 16, 16, 128)
-    repeat(0, 3, z_forward)
-
-    late = gy >= 4
-    first = gy == 0
-    middle = first & (place_z == 0)
-
-    @pl.when(first)
-    def _():
-        kn.wait_recv()
-
-    for load in loads[2:4]:
-        load.wait()
-
-    def prepare(cc):
-        for v in range(2):
-            own, other = [], []
-            for g in range(8):
-                i = 8 * v + g
-                even = kraw[cc, i, pl.ds(0, 16, stride=2), :]
-                even = jnp.where(late, kraw[cc, i, pl.ds(2, 16, stride=2), :], even)
-                odd = kraw[cc, i, pl.ds(1, 16, stride=2), :]
-                row = lax.broadcasted_iota(jnp.int32, even.shape, 0)
-                nyquist = jnp.broadcast_to(kn_in[cc, i : i + 1, 0:64], even.shape)
-                nyquist = jnp.where(first, nyquist, even)
-                packed = jnp.where(top == 1, nyquist, even)
-                if i == 0:
-                    packed = jnp.where(middle, 0.5 * (even + nyquist), packed)
-                    kr_out[cc, 0:1, 0:64] = 0.5 * (even - nyquist)[0:1, :]
-                even = jnp.where(row == 0, packed, even)
-                own.append(jnp.where(top == 1, odd, even))
-                other.append(jnp.where(top == 1, even, odd))
-            kp[cc, 2 * top + v] = -INVERSE_COUNT * jnp.concatenate(own, axis=0).T
-            kq[cc, v] = -INVERSE_COUNT * jnp.concatenate(other, axis=0).T
-
-    repeat(0, 6, prepare)
-    repeat(3, 6, z_forward)
-
-    across = {"gx": lax.rem(gx + 2, 4)}
-    shares = [
-        pltpu.make_async_remote_copy(
-            src_ref=src, dst_ref=dst, send_sem=kn_sems.at[n], recv_sem=kn_sems.at[n + 1],
-            device_id=across, device_id_type=MESH,
-        )
-        for n, src, dst in ((2, kq, kp.at[:, pl.ds(2 * top, 2)]), (4, kr_out, kr_in))
-    ]
-    for share in shares:
-        share.start()
-
-    for load in loads[4:]:
+    repeat(0, 6, z_forward)
+    shares[1].start()
+
+    for load in loads[1:]:
         load.wait()
     row = lax.broadcasted_iota(jnp.int32, (128, 128), 0)
     lane = lax.broadcasted_iota(jnp.int32, (128, 128), 1)
@@ -331,7 +323,9 @@
     packed_lane = first & (top == 0) & ((lane & 15) == 0)
     low = (row & 2) == 0
     lone = ((row & 125) == 0, row < 0)
-    partner = lambda z: jnp.where(real, pltpu.roll(z, 112, 1), pltpu.roll(z, 16, 1))
+    from_imag = lambda z: pltpu.roll(z, 112, 1)
+    from_real = lambda z: pltpu.roll(z, 16, 1)
+    partner = lambda z: jnp.where(real, from_imag(z), from_real(z))
 
     def y_forward(c):
         arrived(1, 2 * c, r2_blocks, 16)
@@ -343,13 +337,13 @@
             halves_x.append(jnp.concatenate([a + b, a - b], axis=1))
         out = [[], []]
         for parity, value in enumerate((halves_x[0] + halves_x[1], halves_x[0] - halves_x[1])):
-            rows = left_product(tabyf, parity, value)
+            rows = wide_product(tabyf, parity, value)
             for e in range(2):
                 cosine, sine = rows[:128, 128 * e : 128 * e + 128], rows[128:, 128 * e : 128 * e + 128]
                 turned = partner(sine)
                 plain = cosine + jnp.where(real, turned, -turned)
                 single = jnp.where(
-                    low, jnp.where(real, cosine, -turned), jnp.where(real, partner(cosine), -sine)
+                    low, jnp.where(real, cosine, -turned), jnp.where(real, from_imag(cosine), -sine)
                 )
                 out[e].append(jnp.where(packed_lane & ~lone[parity], single, plain))
         for e in range(2):
@@ -365,27 +359,50 @@
     def x_forward(c):
         both_arrived(2, c, r3)
         tiles = [r3[c, :, :, 8 * v : 8 * v + 8, :].reshape(128, 128) for v in range(4)]
+        out = left_product(tabx, XF, jnp.concatenate(tiles, axis=1))
         for v in range(4):
-            spec[c, v] = left_product(tabx, XF, tiles[v])
+            spec[c, v] = out[:, 128 * v : 128 * v + 128]
+        out = left_product(tabx, XM, jnp.concatenate(tiles[::2], axis=1))
         for j in range(2):
-            spec[c, 4 + j] = left_product(tabx, XM, tiles[2 * j])
+            spec[c, 4 + j] = out[:, 128 * j : 128 * j + 128]
 
     repeat(0, 2, x_forward)
 
-    for share in shares:
-        share.wait_recv()
-    corner_lane = middle & (top == 0) & (lax.broadcasted_iota(jnp.int32, (64, 128), 1) == 0)
-    for cc in range(6):
-        for j, source in enumerate((kr_out, kr_in)):
-            column = jnp.broadcast_to(source[cc, 0:1, 0:64], (128, 64)).T
-            column = -INVERSE_COUNT * column + (2.0 * EXCHANGE * INVERSE_COUNT if cc < 3 else 0.0)
-            k2[cc, j] = jnp.where(corner_lane, column, 0.0)
-        if cc < 3:
+    for piece in shares:
+        piece.wait_recv()
+    k2[...] = jnp.zeros_like(k2)
+
+    @pl.when(first & (top == 0))
+    def _():
+        for n in range(2):
+            nyquist(n).wait_recv()
+        small_lane = lax.broadcasted_iota(jnp.int32, (64, 128), 1)
+        corner_lane = (place_z == 0) & (small_lane == 0)
+
+        def mend(cc):
             for v in range(4):
-                kp[cc, v] += INVERSE_COUNT * (lamx[...] + lam[v : v + 1, :])
+                rows = [
+                    jnp.broadcast_to(kn_in[v // 2, cc, i : i + 1, 0:64], (16, 64))
+                    for i in range(8 * (v % 2), 8 * (v % 2) + 8)
+                ]
+                edge = -INVERSE_COUNT * jnp.concatenate(rows, axis=0).T
+                plain = kp[cc, v]
+                value = jnp.where((small_lane & 15) == 0, edge, plain) if v >= 2 else plain
+                if v % 2 == 0:
+                    value = jnp.where(corner_lane, 0.5 * (plain + edge), value)
+                    term = jnp.where(cc < 3, 2.0 * EXCHANGE * INVERSE_COUNT, 0.0)
+                    k2[cc, v // 2] = jnp.where(corner_lane, 0.5 * (plain - edge) + term, 0.0)
+                kp[cc, v] = value
+
+        repeat(0, 6, mend)
+
+    for cc in range(3):
+        for v in range(4):
+            kp[cc, v] += INVERSE_COUNT * (lamx[...] + lam[v : v + 1, :])
     x_forward(2)
 
     for c in range(3):
+        tiles = []
         for v in range(4):
             terms = []
             for part in range(2):
@@ -396,8 +413,10 @@
                         k2[PAIR[c][d], v // 2] * spec[d, 4 + v // 2, rows, :] for d in range(3)
                     )
                 terms.append(total)
-            out = left_product(tabx, XB, jnp.concatenate(terms, axis=0))
-            s4[c, :, :, 8 * v : 8 * v + 8, :] = out.reshape(2, 8, 8, 128)
+            tiles.append(jnp.concatenate(terms, axis=0))
+        out = left_product(tabx, XB, jnp.concatenate(tiles, axis=1))
+        for v in range(4):
+            s4[c, :, :, 8 * v : 8 * v + 8, :] = out[:, 128 * v : 128 * v + 128].reshape(2, 8, 8, 128)
         send_both(3, c, s4, r4_blocks)
 
     alternate = (1 - 2 * (row & 1)).astype(F32)
@@ -410,9 +429,9 @@
             value = [
                 jnp.concatenate([pieces[e][2 * g + parity] for g in range(4)], axis=0) for e in range(2)
             ]
-            masked = [jnp.where(low & ~lone[parity], z, 0.0) for z in value]
-            rows = left_product(tabyb, parity, jnp.concatenate(value, axis=1))
-            rows_low = left_product(tabyb, parity, jnp.concatenate(masked, axis=1))
+            masked = jnp.concatenate([jnp.where(low & ~lone[parity], z, 0.0) for z in value], axis=1)
+            rows = wide_product(tabyb, parity, jnp.concatenate(value, axis=1))
+            rows_low = wide_product(tabyb, parity, masked)
             for e in range(2):
                 cols = slice(128 * e, 128 * e + 128)
                 cosine, sine = rows[:128, cols], rows[128:, cols]
@@ -424,7 +443,7 @@
                 if parity == 0:
                     base = value[e][0:1, :] + alternate * value[e][2:3, :]
                     cosine_high = cosine_high - base
-                double = jnp.where(real, cosine_low - partner(sine_low), partner(cosine_high) - sine_high)
+                double = jnp.where(real, cosine_low - from_imag(sine_low), from_real(cosine_high) - sine_high)
                 out[e].append(jnp.where(packed_lane, 2.0 * double + base, plain))
         for h in range(2):
             even, odd = [out[e][0] + out[e][1] if h == 0 else out[e][0] - out[e][1] for e in range(2)]
@@ -458,12 +477,12 @@
     sent(2, 3, lambda n: s3_blocks.at[n, :, pl.ds(0, 7)])
     sent(3, 3, lambda n: s4.at[n, :, pl.ds(0, 7)])
     sent(4, 6, lambda n: s5_blocks.at[n, pl.ds(0, 15)])
-    for share in shares:
-        share.wait_send()
+    for piece in shares:
+        piece.wait_send()
 
     @pl.when(gy == 4)
     def _():
-        kn.wait_send()
+        nyquist(top).wait_send()
 
     repeat(0, 6, lambda n: arrived(5, n, r6, 4))
     sent(5, 6, lambda n: s6.at[n, pl.ds(0, 3)])
@@ -505,7 +524,7 @@
     yf, yb = y_tables()
     tabz = np.stack([halves(t) for t in zf + zb])
     taby = np.stack([halves(t) for t in yf + yb])
-    tabx = np.stack([halves(t) for t in x_tables()])
+    tabx = np.stack([left_halves(t) for t in x_tables()])
     lam, lamx = eigen_tables()
     shape = magnetization.shape
     anywhere = pl.BlockSpec(memory_space=pltpu.HBM)
@@ -521,16 +540,14 @@
             vmem(4, 2, 256, 256, dtype=BF16),
             vmem(2, 2, 256, 128, dtype=BF16),
             vmem(2, 2, 256, 128, dtype=BF16),
-            vmem(3, 2, 128, 128, dtype=BF16),
+            vmem(3, 128, 384, dtype=BF16),
             vmem(4, 128),
             vmem(64, 128),
             vmem(6, 4, 64, 128),
             vmem(6, 2, 64, 128),
             vmem(6, 2, 64, 128),
             vmem(6, 16, 128),
-            vmem(6, 16, 128),
-            vmem(6, 8, 128),
-            vmem(6, 8, 128),
+            vmem(2, 6, 16, 128),
             vmem(6, 4, 4, 16, 128),
             vmem(6, 16, 16, 128),
             vmem(6, 8, 2, 16, 128),
@@ -545,7 +562,7 @@
             pltpu.SemaphoreType.DMA((7,)),
             pltpu.SemaphoreType.DMA((6, 6)),
             pltpu.SemaphoreType.DMA((6, 6)),
-            pltpu.SemaphoreType.DMA((6,)),
+            pltpu.SemaphoreType.DMA((7,)),
         ],
         compiler_params=pltpu.CompilerParams(
             collective_id=0, has_side_effects=True, vmem_limit_bytes=62 * 1024 * 1024

time: 58.3 us -> 57.3 us (0.983)
  Pallas kernels: 56.7 us -> 55.6 us
    pallas_call x1, Pallas kernels: 54.9 us -> 53.8 us  [shards(): pl.pallas_call(transform, out_shape=[vmem(*shape), vmem(6, 4, 64, 128)],...]
where the time goes in v5:
time: 57.3 us; the launch traced here: 56.3 us
  Pallas kernels  55.6 us (97%)
  between operations  0.65 us (1%)
    pallas_call x1, Pallas kernels, shards(): pl.pallas_call(transform, out_shape=[vmem(*shape), vmem(6, 4, 64, 128)],...  53.8 us
    pallas_call x1, Pallas kernels, shards(): pl.pallas_call(advance, out_shape=[jax.ShapeDtypeStruct(shape, F32)] * 2,...  1.83 us

profile of v5, /device:TPU:0, one launch (start us, length us, event | category | flops | bytes accessed | tf_op | source)
XLA Modules:
  0.0 56.3 jit_solution(10976020008340807014)
XLA Ops:
  0.6 0.0 copy-start
  0.6 53.8 %shard_map.95 = (f32[3,16,32,128]{3,2,1,0:T(8,128)S(1)}, f32[6,4,64,128]{3,2,1,0:T(8,128)S(1)}) custom-call(f32[3,16,32,128]{3,2,1,0:T(8,128)} %m_hbm.1, f32[6,16,64,64]{3,2,1,0:T(8,128)} %k_hbm.1, bf16[4,2,256,256]{3,2,1,0:T(8,128)(2,1)} %constant.10.clone.tabz_hbm, bf16[4,2,256,128]{3,2,1,0:T(8,128)(2,1)} %constant.11.clone.taby_hbm, ...), custom_call_target="tpu_custom_call" | custom-call | tf_op jit(solution)/shard_map/pallas_call | solution.py:533
  54.4 0.0 copy-done
  54.4 1.8 %shard_map.96 = (f32[3,16,32,128]{3,2,1,0:T(8,128)}, f32[3,16,32,128]{3,2,1,0:T(8,128)}) custom-call(f32[3,16,32,128]{3,2,1,0:T(8,128)S(1)} %get-tuple-element.4.m, f32[6,4,64,128]{3,2,1,0:T(8,128)S(1)} %get-tuple-element.5.demag, f32[3]{0:T(128)S(1)} %copy-done), custom_call_target="tpu_custom_call" | custom-call | tf_op jit(solution)/shard_map/pallas_call | solution.py:574
Async XLA Ops:
  0.6 53.8 %copy-start = (f32[3]{0:T(128)S(1)}, f32[3]{0:T(128)}, u32[]{:S(2)}) copy-start(f32[3]{0:T(128)} %applied.1) | copy-start | bytes 40

commit v6 on v5

--- a/solution.py
+++ b/solution.py
@@ -183,7 +183,7 @@
     on_cz = [
         (4 * k + z, {"gx": 2 * top + k, "gz": z})
         for k, z in (
-            (lax.rem(core + k, 2), lax.rem(gz + d, 4)) for d in (2, 1, 3, 0) for k in (0, 1) if (d, k) != (0, 0)
+            (lax.rem(core + k, 2), lax.rem(gz + d, 4)) for d in (2, 1, 3, 0) for k in (1, 0) if (d, k) != (0, 0)
         )
     ]
 

time: 57.3 us -> 56 us (0.977); the launches traced: 56.3 us -> 55.9 us
  no operation moved by 1% of the time
where the time goes in v6:
time: 56 us; the launch traced here: 55.9 us
  Pallas kernels  55.2 us (99%)
  between operations  0.65 us (1%)
    pallas_call x1, Pallas kernels, shards(): pl.pallas_call(transform, out_shape=[vmem(*shape), vmem(6, 4, 64, 128)],...  53.4 us
    pallas_call x1, Pallas kernels, shards(): pl.pallas_call(advance, out_shape=[jax.ShapeDtypeStruct(shape, F32)] * 2,...  1.83 us

profile of v6, /device:TPU:0, one launch (start us, length us, event | category | flops | bytes accessed | tf_op | source)
XLA Modules:
  0.0 55.9 jit_solution(8965097224656479422)
XLA Ops:
  0.6 0.0 copy-start
  0.6 53.4 %shard_map.95 = (f32[3,16,32,128]{3,2,1,0:T(8,128)S(1)}, f32[6,4,64,128]{3,2,1,0:T(8,128)S(1)}) custom-call(f32[3,16,32,128]{3,2,1,0:T(8,128)} %m_hbm.1, f32[6,16,64,64]{3,2,1,0:T(8,128)} %k_hbm.1, bf16[4,2,256,256]{3,2,1,0:T(8,128)(2,1)} %constant.10.clone.tabz_hbm, bf16[4,2,256,128]{3,2,1,0:T(8,128)(2,1)} %constant.11.clone.taby_hbm, ...), custom_call_target="tpu_custom_call" | custom-call | tf_op jit(solution)/shard_map/pallas_call | solution.py:533
  54.1 0.0 copy-done
  54.1 1.8 %shard_map.96 = (f32[3,16,32,128]{3,2,1,0:T(8,128)}, f32[3,16,32,128]{3,2,1,0:T(8,128)}) custom-call(f32[3,16,32,128]{3,2,1,0:T(8,128)S(1)} %get-tuple-element.4.m, f32[6,4,64,128]{3,2,1,0:T(8,128)S(1)} %get-tuple-element.5.demag, f32[3]{0:T(128)S(1)} %copy-done), custom_call_target="tpu_custom_call" | custom-call | tf_op jit(solution)/shard_map/pallas_call | solution.py:574
Async XLA Ops:
  0.6 53.4 %copy-start = (f32[3]{0:T(128)S(1)}, f32[3]{0:T(128)}, u32[]{:S(2)}) copy-start(f32[3]{0:T(128)} %applied.1) | copy-start | bytes 40

commit v7 on v6

--- a/solution.py
+++ b/solution.py
@@ -350,7 +350,9 @@
             parts = swap_lanes([out[e][g % 2][32 * (g // 2) : 32 * (g // 2) + 32] for g in range(8)])
             for x in range(8):
                 s3[c, e, pl.ds(x, 32, stride=8), :] = parts[x]
-        send_both(2, c, s3_blocks, r3)
+            for p, device in on_cz:
+                copy(2, c, s3_blocks.at[c, e, p], r3.at[c, e, place_z], device).start()
+        r3[c, :, place_z] = s3_blocks[c, :, place_z]
 
     s3_blocks = s3.reshape(3, 2, 8, 32, 128)
     r4_blocks = r4.reshape(3, 2, 8, 32, 128)

time: 56 us -> 56.3 us (level)
  no operation moved by 1% of the time
where the time goes in v7:
time: 56.3 us; the launch traced here: 56.2 us
  Pallas kernels  55.5 us (99%)
  between operations  0.65 us (1%)
    pallas_call x1, Pallas kernels, shards(): pl.pallas_call(transform, out_shape=[vmem(*shape), vmem(6, 4, 64, 128)],...  53.7 us
    pallas_call x1, Pallas kernels, shards(): pl.pallas_call(advance, out_shape=[jax.ShapeDtypeStruct(shape, F32)] * 2,...  1.83 us

profile of v7, /device:TPU:0, one launch (start us, length us, event | category | flops | bytes accessed | tf_op | source)
XLA Modules:
  0.0 56.2 jit_solution(16056099330792769655)
XLA Ops:
  0.6 0.0 copy-start
  0.6 53.7 %shard_map.95 = (f32[3,16,32,128]{3,2,1,0:T(8,128)S(1)}, f32[6,4,64,128]{3,2,1,0:T(8,128)S(1)}) custom-call(f32[3,16,32,128]{3,2,1,0:T(8,128)} %m_hbm.1, f32[6,16,64,64]{3,2,1,0:T(8,128)} %k_hbm.1, bf16[4,2,256,256]{3,2,1,0:T(8,128)(2,1)} %constant.10.clone.tabz_hbm, bf16[4,2,256,128]{3,2,1,0:T(8,128)(2,1)} %constant.11.clone.taby_hbm, ...), custom_call_target="tpu_custom_call" | custom-call | tf_op jit(solution)/shard_map/pallas_call | solution.py:535
  54.3 0.0 copy-done
  54.3 1.8 %shard_map.96 = (f32[3,16,32,128]{3,2,1,0:T(8,128)}, f32[3,16,32,128]{3,2,1,0:T(8,128)}) custom-call(f32[3,16,32,128]{3,2,1,0:T(8,128)S(1)} %get-tuple-element.4.m, f32[6,4,64,128]{3,2,1,0:T(8,128)S(1)} %get-tuple-element.5.demag, f32[3]{0:T(128)S(1)} %copy-done), custom_call_target="tpu_custom_call" | custom-call | tf_op jit(solution)/shard_map/pallas_call | solution.py:576
Async XLA Ops:
  0.6 53.7 %copy-start = (f32[3]{0:T(128)S(1)}, f32[3]{0:T(128)}, u32[]{:S(2)}) copy-start(f32[3]{0:T(128)} %applied.1) | copy-start | bytes 40
